TPU v7x, 32 devices: a whole 2x2x4 slice. The times are simulated.
32 devices in a mesh: seq: 16 (over z, y, x), head: 2 (over core).
Axes of the slice: x: 2, y: 2, z: 4, core: 2. Of those that a mesh axis runs over, the one named last changes fastest.
Arguments:
- acceptance_signal: bfloat16 [8192, 2048], P(('seq', 'head')), may hold values from -6 to 6
- lookup_entries: bfloat16 [8192, 2048], P(('seq', 'head')), may hold values from -6 to 6
- content_entries: bfloat16 [8192, 2048], P(('seq', 'head')), may hold values from -6 to 6
- fading_exponent_table: bfloat16 [8192, 2048], P(('seq', 'head')), may hold values from -17 to 0
- raw_control_signal: bfloat16 [8192, 2048], P(('seq', 'head')), may hold values from -6 to 6
- current_token_reward: float32 [32, 64], P('head'), may hold values from -1 to 1
- slice_scaling_factor: float32 [2048], P('head'), may hold values from 0.1 to 1.9
- result_mapping: bfloat16 [2048, 4096], P('head'), may hold values from -0.125 to 0.125
Outputs:
- time_mixed: bfloat16 [8192, 4096], P(('seq', 'head'))
All inputs are finite; a program needn't handle non-finite values.
Results may differ from a plain program's by a relative error of at most 0.009.
Values may be sent and summed in bfloat16 or wider, within the bound.
A program may use at most 192 MiB of HBM per device.

v0:
```python
import functools

import jax
import jax.numpy as jnp
from jax import lax
from jax.experimental import pallas as pl
from jax.experimental.pallas import tpu as pltpu
from jax.sharding import PartitionSpec as P

BLOCK = 128
LANES = 128
QUAD = 256
CHUNK = 512
EPS = 1e-05
MESH = pl.DeviceIdType.MESH
F32 = jnp.float32
BF16 = jnp.bfloat16


def dot(a, b):
    return jnp.dot(a, b, preferred_element_type=F32)


def dot_nt(a, b):
    return lax.dot_general(a, b, (((1,), (1,)), ((), ())), preferred_element_type=F32)


def dot_tn(a, b):
    return lax.dot_general(a, b, (((0,), (0,)), ((), ())), preferred_element_type=F32)


def split_heads(x, low):
    zero = jnp.zeros_like(x)
    return jnp.concatenate([jnp.where(low, x, zero), jnp.where(low, zero, x)], axis=0)


def kernel(
    n, breadth,
    rec_hbm, key_hbm, val_hbm, fade_hbm, gate_hbm, reward_ref, gain_ref, map_hbm,
    out_hbm,
    fade, key, val, rec, gate, weight, rec_mid, key_mid, local_out, entering, pref_row, mid_row,
    outbox, outdec, inbox, indec, outbox2, carry, gated, snd, rcv, outv,
    in_send, in_recv, in_local, w_sem, s_send, s_recv, d_send, d_recv, c_send, c_recv,
    p_send, p_recv, o_sem,
):
    me, core = lax.axis_index("seq"), lax.axis_index("head")
    other = 1 - core
    rows, width = rec_hbm.shape[0], rec.shape[1]
    tokens = rec.shape[0]
    blocks, quads, pairs = tokens // BLOCK, width // QUAD, width // LANES
    chunks = weight.shape[0]
    piece = outbox.shape[1]
    per_pair = breadth // piece
    my_rows = pl.ds(pl.multiple_of(core * rows, 128), rows)
    their_rows = pl.ds(pl.multiple_of(other * rows, 128), rows)
    my_cols = pl.ds(pl.multiple_of(core * width, 128), width)
    their_cols = pl.ds(pl.multiple_of(other * width, 128), width)
    pairs_io = ((fade_hbm, fade), (key_hbm, key), (val_hbm, val), (rec_hbm, rec), (gate_hbm, gate))

    locals_ = [
        pltpu.make_async_copy(src.at[:, my_cols], dst.at[my_rows, :], in_local.at[i])
        for i, (src, dst) in enumerate(pairs_io)
    ]
    remotes = [
        pltpu.make_async_remote_copy(
            src_ref=src.at[:, their_cols], dst_ref=dst.at[my_rows, :],
            send_sem=in_send.at[i], recv_sem=in_recv.at[i],
            device_id=(me, other), device_id_type=MESH,
        )
        for i, (src, dst) in enumerate(pairs_io)
    ]
    barrier = pltpu.get_barrier_semaphore()
    pl.semaphore_signal(barrier, inc=1, device_id=(me, other), device_id_type=MESH)

    def greet(d, c):
        pl.semaphore_signal(
            barrier, inc=1, device_id=(lax.rem(me + d, n), core), device_id_type=MESH
        )
        return c

    lax.fori_loop(1, n, greet, 0)
    for copy in locals_:
        copy.start()
    pl.semaphore_wait(barrier, n)
    for copy in remotes:
        copy.start()

    def weight_copy(c):
        return pltpu.make_async_copy(
            map_hbm.at[:, pl.ds(pl.multiple_of(c * CHUNK, CHUNK), CHUNK)], weight.at[c], w_sem.at[c]
        )

    for c in range(chunks):
        weight_copy(c).start()

    t_id = lax.broadcasted_iota(jnp.int32, (BLOCK, 2 * BLOCK), 0)
    s_id = lax.rem(lax.broadcasted_iota(jnp.int32, (BLOCK, 2 * BLOCK), 1), BLOCK)
    incl = jnp.where(t_id >= s_id, 1.0, 0.0).astype(BF16)
    low = lax.broadcasted_iota(jnp.int32, (BLOCK, LANES), 1) < breadth
    low_s = lax.broadcasted_iota(jnp.int32, (breadth, LANES), 1) < breadth
    head_i = lax.broadcasted_iota(jnp.int32, (LANES, LANES), 0) // breadth
    head_j = lax.broadcasted_iota(jnp.int32, (LANES, LANES), 1) // breadth
    ones = jnp.where(head_i == head_j, 1.0, 0.0).astype(BF16)
    means = jnp.where(head_i == head_j, 1.0 / breadth, 0.0).astype(BF16)

    for i in range(4):
        locals_[i].wait()
        remotes[i].wait_recv()

    def decays(q, c):
        lanes = pl.ds(pl.multiple_of(q * QUAD, QUAD), QUAD)
        states = [jnp.zeros((breadth, LANES), F32) for _ in range(2)]
        pref = jnp.zeros((1, QUAD), F32)
        for b in range(blocks):
            at = pl.ds(b * BLOCK, BLOCK)
            log_decay = -jnp.exp(fade[at, lanes].astype(F32))
            hi = log_decay.astype(BF16)
            lo = (log_decay - hi.astype(F32)).astype(BF16)
            cum = dot(incl, jnp.concatenate([hi, lo], axis=0))
            mid, total = cum[BLOCK // 2 - 1 : BLOCK // 2], cum[BLOCK - 1 :]
            km = (key[at, lanes].astype(F32) * jnp.exp(mid - cum)).astype(BF16)
            rec_mid[at, lanes] = (
                rec[at, lanes].astype(F32) * jnp.exp(cum - log_decay - mid)
            ).astype(BF16)
            key_mid[at, lanes] = km
            pref_row[b, :, lanes] = pref
            mid_row[b, :, lanes] = mid
            vb = val[at, lanes]
            end, whole = jnp.exp(total - mid), jnp.exp(total)
            for j in range(2):
                cut = slice(j * LANES, (j + 1) * LANES)
                entering[b, 2 * q + j] = states[j]
                product = dot_tn(vb[:, cut], km[:, cut])
                own = jnp.where(low_s, product[:breadth], product[breadth:])
                states[j] = states[j] * whole[:, cut] + own * end[:, cut]
            pref = pref + total
        for j in range(2):
            cut = slice(j * LANES, (j + 1) * LANES)
            for s in range(per_pair):
                slot = (2 * q + j) * per_pair + s
                outbox[slot] = states[j][s * piece : (s + 1) * piece].astype(BF16)
                outdec[slot] = pref[:, cut]
        return c

    lax.fori_loop(0, quads, decays, 0)

    inbox[me] = outbox[me]
    indec[me] = outdec[me]

    def state_copies(d):
        peer = lax.rem(me + d, n)
        return (
            pltpu.make_async_remote_copy(
                src_ref=outbox.at[peer], dst_ref=inbox.at[me],
                send_sem=s_send.at[d], recv_sem=s_recv.at[d],
                device_id=(peer, core), device_id_type=MESH,
            ),
            pltpu.make_async_remote_copy(
                src_ref=outdec.at[peer], dst_ref=indec.at[me],
                send_sem=d_send.at[d], recv_sem=d_recv.at[d],
                device_id=(peer, core), device_id_type=MESH,
            ),
        )

    def carry_copy(d):
        peer = lax.rem(me + d, n)
        return pltpu.make_async_remote_copy(
            src_ref=outbox2.at[peer], dst_ref=carry.at[me],
            send_sem=c_send.at[d], recv_sem=c_recv.at[d],
            device_id=(peer, core), device_id_type=MESH,
        )

    def send_states(d, c):
        for copy in state_copies(d):
            copy.start()
        return c

    lax.fori_loop(1, n, send_states, 0)

    def within(q, c):
        for j in range(2):
            lanes = pl.ds(pl.multiple_of(q * QUAD + j * LANES, LANES), LANES)
            reward = reward_ref[:, lanes]
            for b in range(blocks):
                at = pl.ds(b * BLOCK, BLOCK)
                vb = val[at, lanes]
                scores = dot_nt(rec_mid[at, lanes], split_heads(key_mid[at, lanes], low))
                scores = jnp.where(t_id > s_id, scores, 0.0).astype(BF16)
                own = rec[at, lanes].astype(F32) * key[at, lanes].astype(F32) * reward
                local_out[at, lanes] = dot(scores, split_heads(vb, low)) + dot(
                    own.astype(BF16), ones
                ) * vb.astype(F32)
        return c

    half = quads // 2
    lax.fori_loop(0, half, within, 0)

    def wait_states(d, c):
        for copy in state_copies(d):
            copy.wait()
        return c

    lax.fori_loop(1, n, wait_states, 0)

    def scan(i, run):
        outbox2[i] = run.astype(BF16)
        return run * jnp.exp(indec[i]) + inbox[i].astype(F32)

    lax.fori_loop(0, n, scan, jnp.zeros((piece, LANES), F32))
    carry[me] = outbox2[me]

    def send_carry(d, c):
        carry_copy(d).start()
        return c

    lax.fori_loop(1, n, send_carry, 0)
    lax.fori_loop(half, quads, within, 0)
    locals_[4].wait()
    remotes[4].wait_recv()

    def wait_carry(d, c):
        carry_copy(d).wait()
        return c

    lax.fori_loop(1, n, wait_carry, 0)

    def finish(q, c):
        for j in range(2):
            pair = 2 * q + j
            lanes = pl.ds(pl.multiple_of(q * QUAD + j * LANES, LANES), LANES)
            gain = gain_ref[:, lanes]
            came = jnp.concatenate(
                [carry[pair * per_pair + s].astype(F32) for s in range(per_pair)], axis=0
            )
            for b in range(blocks):
                at = pl.ds(b * BLOCK, BLOCK)
                state = entering[b, pair] + jnp.exp(pref_row[b, :, lanes]) * came
                state = (state * jnp.exp(mid_row[b, :, lanes])).astype(BF16)
                o = local_out[at, lanes] + dot_nt(rec_mid[at, lanes], split_heads(state, low_s))
                hi = o.astype(BF16)
                lo = (o - hi.astype(F32)).astype(BF16)
                centred = o - (dot(hi, means) + dot(lo, means))
                var = dot((centred * centred).astype(BF16), means)
                g = gate[at, lanes].astype(F32)
                normed = centred * lax.rsqrt(var + EPS) * gain
                gated[at, lanes] = (normed * (g / (1.0 + jnp.exp(-g)))).astype(BF16)
        return c

    lax.fori_loop(0, quads, finish, 0)

    def part_copy(c):
        return pltpu.make_async_remote_copy(
            src_ref=snd.at[c], dst_ref=rcv.at[c],
            send_sem=p_send.at[c], recv_sem=p_recv.at[c],
            device_id=(me, other), device_id_type=MESH,
        )

    def out_copy(c):
        return pltpu.make_async_copy(
            outv.at[c], out_hbm.at[:, pl.ds(pl.multiple_of(c * CHUNK, CHUNK), CHUNK)], o_sem.at[c]
        )

    def give(c, x):
        weight_copy(c).wait()
        snd[c] = dot(gated[their_rows, :], weight[c]).astype(BF16)
        part_copy(c).start()
        return x

    lax.fori_loop(0, chunks, give, 0)

    def take(c, x):
        mine = dot(gated[my_rows, :], weight[c])
        part_copy(c).wait_recv()
        outv[c] = (mine + rcv[c].astype(F32)).astype(BF16)
        out_copy(c).start()
        return x

    lax.fori_loop(0, chunks, take, 0)

    def drain(c, x):
        part_copy(c).wait_send()
        out_copy(c).wait()
        return x

    lax.fori_loop(0, chunks, drain, 0)
    for copy in remotes:
        copy.wait_send()


def shards(n, rec, key, val, fade, gate, reward, gain, mapping):
    rows = rec.shape[0]
    breadth = reward.shape[1]
    width = mapping.shape[0]
    depth = mapping.shape[1]
    tokens = rows * rec.shape[1] // width
    blocks, pairs, chunks = tokens // BLOCK, width // LANES, depth // CHUNK
    piece = pairs * breadth // n
    held = pltpu.VMEM((tokens, width), BF16)
    dma = pltpu.SemaphoreType.DMA
    anywhere = pl.BlockSpec(memory_space=pl.ANY)
    vmem = pl.BlockSpec(memory_space=pltpu.VMEM)
    return pl.pallas_call(
        functools.partial(kernel, n, breadth),
        out_shape=jax.ShapeDtypeStruct((rows, depth), BF16),
        in_specs=[anywhere] * 5 + [vmem] * 2 + [anywhere],
        out_specs=anywhere,
        scratch_shapes=[
            held, held, held, held, held,
            pltpu.VMEM((chunks, width, CHUNK), BF16),
            held, held,
            pltpu.VMEM((tokens, width), F32),
            pltpu.VMEM((blocks, pairs, breadth, LANES), F32),
            pltpu.VMEM((blocks, 1, width), F32),
            pltpu.VMEM((blocks, 1, width), F32),
            pltpu.VMEM((n, piece, LANES), BF16),
            pltpu.VMEM((n, 1, LANES), F32),
            pltpu.VMEM((n, piece, LANES), BF16),
            pltpu.VMEM((n, 1, LANES), F32),
            pltpu.VMEM((n, piece, LANES), BF16),
            pltpu.VMEM((n, piece, LANES), BF16),
            held,
            pltpu.VMEM((chunks, rows, CHUNK), BF16),
            pltpu.VMEM((chunks, rows, CHUNK), BF16),
            pltpu.VMEM((chunks, rows, CHUNK), BF16),
            dma((5,)), dma((5,)), dma((5,)), dma((chunks,)),
            dma((n,)), dma((n,)), dma((n,)), dma((n,)), dma((n,)), dma((n,)),
            dma((chunks,)), dma((chunks,)), dma((chunks,)),
        ],
        compiler_params=pltpu.CompilerParams(
            collective_id=0, has_side_effects=True, vmem_limit_bytes=56 * 2**20
        ),
    )(rec, key, val, fade, gate, reward.reshape(1, -1), gain.reshape(1, -1), mapping)


def solution(mesh):
    tokens = P(("seq", "head"), None)
    placed = (tokens,) * 5 + (P("head", None), P("head"), P("head", None))
    return jax.shard_map(
        functools.partial(shards, mesh.shape["seq"]),
        mesh=mesh, in_specs=placed, out_specs=tokens, check_vma=False,
    )
```

profile of v0, /device:TPU:0, one launch (start us, length us, event | category | flops | bytes accessed | tf_op | source)
XLA Modules:
  0.0 45.9 jit_solution(12045342408852570218)
XLA Ops:
  0.0 1.4 %reshape.6.reward_ref = f32[1,1024]{1,0:T(1,128)} reshape(f32[16,64]{1,0:T(8,128)} %param.13) | data formatting | bytes 8192 | tf_op jit(solution)/shard_map/reshape | solution.py:332
  1.4 41.3 %shard_map.82 = bf16[256,4096]{1,0:T(8,128)(2,1)} custom-call(bf16[256,2048]{1,0:T(8,128)(2,1)} %rec_hbm.1, bf16[256,2048]{1,0:T(8,128)(2,1)} %key_hbm.1, bf16[256,2048]{1,0:T(8,128)(2,1)} %val_hbm.1, bf16[256,2048]{1,0:T(8,128)(2,1)} %fade_hbm.1, bf16[256,2048]{1,0:T(8,128)(2,1)} %gate_hbm.1, f32[1,1024]{1,0:T(1,128)} %reshape.6.reward_ref, ...), custom_call_target="tpu_custom_call" | custom-call | tf_op jit(solution)/shard_map/pallas_call | solution.py:302
  42.7 3.1 %copy.10 = bf16[256,4096]{1,0:T(8,128)(2,1)} copy(bf16[256,4096]{1,0:T(8,128)(2,1)} %shard_map.82) | data formatting | bytes 4194304
where the time goes:
time: 46.1 us; the launch traced here: 45.9 us
  Pallas kernels  41.3 us (90%)
  local copies, waits for them, and re-layouts  4.49 us (10%)
    pallas_call x1, Pallas kernels, shards(): pl.pallas_call(functools.partial(kernel, n, breadth), out_shape=jax.Shape...  41.3 us
    unnamed x1, local copies, waits for them, and re-layouts  3.13 us
    reshape x1, local copies, waits for them, and re-layouts, shards(): reward.reshape(1, -1)  1.36 us

commit v1 on v0

v1 whole, which is shorter than its diff:
```python
import functools

import jax
import jax.numpy as jnp
from jax import lax
from jax.experimental import pallas as pl
from jax.experimental.pallas import tpu as pltpu
from jax.sharding import PartitionSpec as P

BLOCK = 128
LANES = 128
QUAD = 256
CHUNK = 512
EXTRA = 16
EPS = 1e-05
MESH = pl.DeviceIdType.MESH
F32 = jnp.float32
BF16 = jnp.bfloat16


def dot(a, b):
    return jnp.dot(a, b, preferred_element_type=F32)


def dot_nt(a, b):
    return lax.dot_general(a, b, (((1,), (1,)), ((), ())), preferred_element_type=F32)


def dot_tn(a, b):
    return lax.dot_general(a, b, (((0,), (0,)), ((), ())), preferred_element_type=F32)


def split_heads(x, low):
    zero = jnp.zeros_like(x)
    return jnp.concatenate([jnp.where(low, x, zero), jnp.where(low, zero, x)], axis=0)


def flip(r, i, members):
    q, bit = 0, 1
    while bit < members:
        q = q + bit * (((r // bit) % 2 + (i // bit) % 2) % 2)
        bit *= 2
    return q


def kernel(
    n, cores, breadth,
    rec_hbm, key_hbm, val_hbm, fade_hbm, gate_hbm, reward_hbm, gain_hbm, map_hbm,
    out_ref,
    fade, key, val, rec, gate, rewards, gains, weight,
    reward_row, cumx, key_mid, centred, recs, local_out, swish, entering, pref_row, mid_row,
    outbox, inbox, before, before_dec, gout, gin, cbox, carry, gated,
    in_sem, p_local, p_send, p_recv, w_sem, w_send, w_recv,
    s_send, s_recv, g_send, g_recv, c_send, c_recv, ready,
):
    me, core = lax.axis_index("seq"), lax.axis_index("head")
    other = 1 - core
    tokens, width = fade.shape
    blocks, quads = tokens // BLOCK, width // QUAD
    half = width // cores
    chunks = weight.shape[1]
    members = quads
    span = members // cores
    groups = n // span
    group = me // span
    r = (me % span) * cores + core

    def place(q):
        return (group * span + q // cores, q % cores)

    def above(g):
        return (g * span + me % span, core)

    sources = (fade_hbm, key_hbm, val_hbm, rec_hbm, gate_hbm)
    held = (fade, key, val, rec, gate)
    first = (1 - r // (members // 2)) * (width // 2)
    second = (r // (members // 2)) * (width // 2)

    def load(i, part):
        at = pl.ds(pl.multiple_of((first, second)[part], LANES), width // 2)
        return pltpu.make_async_copy(
            sources[i].at[:, at], held[i].at[:, at], in_sem.at[2 * i + part]
        )

    for part in range(2):
        for i in range(3):
            load(i, part).start()

    barrier = pltpu.get_barrier_semaphore()

    def greet(i, c):
        pl.semaphore_signal(
            barrier, inc=1, device_id=place(flip(r, i, members)), device_id_type=MESH
        )
        return c

    def greet_above(g, c):
        pl.semaphore_signal(barrier, inc=1, device_id=above(g), device_id_type=MESH)
        return c

    lax.fori_loop(1, members, greet, 0)
    lax.fori_loop(group + 1, groups, greet_above, 0)
    for i in range(3, 5):
        for part in range(2):
            load(i, part).start()

    small = ((reward_hbm, rewards), (gain_hbm, gains))
    small_local = [
        pltpu.make_async_copy(src, dst.at[core], p_local.at[i]) for i, (src, dst) in enumerate(small)
    ]
    small_remote = [
        pltpu.make_async_remote_copy(
            src_ref=src, dst_ref=dst.at[core], send_sem=p_send.at[i], recv_sem=p_recv.at[i],
            device_id=(me, other), device_id_type=MESH,
        )
        for i, (src, dst) in enumerate(small)
    ]
    small_in = [
        pltpu.make_async_remote_copy(
            src_ref=src, dst_ref=dst.at[other], send_sem=p_send.at[i], recv_sem=p_recv.at[i],
            device_id=(me, other), device_id_type=MESH,
        )
        for i, (src, dst) in enumerate(small)
    ]
    for copy in small_local:
        copy.start()

    def columns(k):
        return map_hbm.at[:, pl.ds(pl.multiple_of(k * CHUNK, CHUNK), CHUNK)]

    def weight_local(k):
        return pltpu.make_async_copy(columns(k), weight.at[core, k], w_sem.at[k])

    def weight_remote(k, side):
        return pltpu.make_async_remote_copy(
            src_ref=columns(k), dst_ref=weight.at[side, k],
            send_sem=w_send.at[k], recv_sem=w_recv.at[k],
            device_id=(me, other), device_id_type=MESH,
        )

    def send_weight(start, stop):
        for k in range(start, min(stop, chunks)):
            weight_remote(k, core).start()

    t_id = lax.broadcasted_iota(jnp.int32, (BLOCK, 2 * BLOCK), 0)
    s_id = lax.rem(lax.broadcasted_iota(jnp.int32, (BLOCK, 2 * BLOCK), 1), BLOCK)
    incl = jnp.where(t_id >= s_id, 1.0, 0.0).astype(BF16)
    low = lax.broadcasted_iota(jnp.int32, (BLOCK, LANES), 1) < breadth
    low_s = lax.broadcasted_iota(jnp.int32, (breadth, LANES), 1) < breadth
    row_x = lax.broadcasted_iota(jnp.int32, (EXTRA, LANES), 0)

    def same_head(size):
        i = lax.broadcasted_iota(jnp.int32, (size, size), 0)
        j = lax.broadcasted_iota(jnp.int32, (size, size), 1)
        return i // breadth == j // breadth, i == j

    same, equal = same_head(QUAD)
    means = jnp.where(same, 1.0 / breadth, 0.0).astype(BF16)
    centre = (jnp.where(equal, 1.0, 0.0) - jnp.where(same, 1.0 / breadth, 0.0)).astype(BF16)
    ones = jnp.where(same, 1.0, 0.0).astype(BF16)

    def pack_rows(dec):
        hi = dec.astype(BF16).astype(F32)
        lo = dec - hi
        rows = (hi[:, :LANES], lo[:, :LANES], hi[:, LANES:], lo[:, LANES:])
        out = jnp.zeros((EXTRA, LANES), F32)
        for i, row in enumerate(rows):
            out = jnp.where(row_x == i, row, out)
        return out.astype(BF16)

    def unpack_rows(x):
        x = x.astype(F32)
        return x[0:1] + x[1:2], x[2:3] + x[3:4]

    def member_copy(src, dst, j, slot, send, recv):
        return pltpu.make_async_remote_copy(
            src_ref=src.at[j], dst_ref=dst.at[slot], send_sem=send.at[j], recv_sem=recv.at[slot],
            device_id=place(j), device_id_type=MESH,
        )

    def decays(step, c):
        i = members - 1 - step
        q = flip(r, i, members)
        lanes = pl.ds(pl.multiple_of(q * QUAD, QUAD), QUAD)
        states = [jnp.zeros((breadth, LANES), F32) for _ in range(2)]
        pref = jnp.zeros((1, QUAD), F32)
        for b in range(blocks):
            at = pl.ds(b * BLOCK, BLOCK)
            log_decay = -jnp.exp(fade[at, lanes].astype(F32))
            hi = log_decay.astype(BF16)
            lo = (log_decay - hi.astype(F32)).astype(BF16)
            cum = dot(incl, jnp.concatenate([hi, lo], axis=0))
            mid, total = cum[BLOCK // 2 - 1 : BLOCK // 2], cum[BLOCK - 1 :]
            km = (key[at, lanes].astype(F32) * jnp.exp(mid - cum)).astype(BF16)
            vb = dot(val[at, lanes], centre).astype(BF16)
            cumx[at, lanes] = cum - log_decay
            key_mid[at, lanes] = km
            centred[at, lanes] = vb
            pref_row[b, :, lanes] = pref
            mid_row[b, :, lanes] = mid
            end, whole, begin = jnp.exp(total - mid), jnp.exp(total), jnp.exp(mid)
            for j in range(2):
                cut = slice(j * LANES, (j + 1) * LANES)
                if b > 0:
                    entering[b - 1, 2 * q + j] = (states[j] * begin[:, cut]).astype(BF16)
                product = dot_tn(vb[:, cut], km[:, cut])
                own = jnp.where(low_s, product[:breadth], product[breadth:])
                states[j] = states[j] * whole[:, cut] + own * end[:, cut]
            pref = pref + total
        for j in range(2):
            outbox[q, pl.ds(j * breadth, breadth), :] = states[j].astype(BF16)
        outbox[q, pl.ds(2 * breadth, EXTRA), :] = pack_rows(jnp.exp(pref))

        @pl.when(i > 0)
        def _():
            member_copy(outbox, inbox, q, r, s_send, s_recv).start()

        return c

    def within(step, c):
        q = flip(r, step, members)
        lanes = pl.ds(pl.multiple_of(q * QUAD, QUAD), QUAD)
        gain = gains[q // span, :, pl.ds(pl.multiple_of((q % span) * QUAD, QUAD), QUAD)]
        reward = reward_row[:, lanes]
        for b in range(blocks):
            at = pl.ds(b * BLOCK, BLOCK)
            g = gate[at, lanes].astype(F32)
            swish[at, lanes] = g / (1.0 + jnp.exp(-g)) * gain
            cx = cumx[at, lanes]
            rf = rec[at, lanes].astype(F32)
            kb, vb = key_mid[at, lanes], centred[at, lanes]
            rm = (rf * jnp.exp(cx - mid_row[b, :, lanes])).astype(BF16)
            recs[at, lanes] = (rf * jnp.exp(cx + pref_row[b, :, lanes])).astype(BF16)
            own = rf * key[at, lanes].astype(F32) * reward
            diag = dot(own.astype(BF16), ones)
            for j in range(2):
                cut = slice(j * LANES, (j + 1) * LANES)
                scores = dot_nt(rm[:, cut], split_heads(kb[:, cut], low))
                scores = jnp.where(t_id > s_id, scores, 0.0).astype(BF16)
                o = dot(scores, split_heads(vb[:, cut], low)) + diag[:, cut] * vb[:, cut].astype(F32)
                if b > 0:
                    o = o + dot_nt(rm[:, cut], split_heads(entering[b - 1, 2 * q + j], low_s))
                local_out[at, pl.ds(pl.multiple_of(q * QUAD + j * LANES, LANES), LANES)] = o
        return c

    with jax.named_scope("in0"):
        for i in range(3):
            load(i, 0).wait()
    with jax.named_scope("barrier"):
        pl.semaphore_wait(barrier, members - 1 + group)
        for copy in small_remote:
            copy.start()

        def here(g, c):
            pl.semaphore_signal(ready, inc=1, device_id=above(g), device_id_type=MESH)
            return c

        lax.fori_loop(0, group, here, 0)
        send_weight(0, 2)
        for k in range(chunks):
            weight_local(k).start()
    with jax.named_scope("decays0"):
        lax.fori_loop(0, members // 2, decays, 0)
    with jax.named_scope("in1"):
        for i in range(3):
            load(i, 1).wait()
    with jax.named_scope("decays1"):
        lax.fori_loop(members // 2, members, decays, 0)
    send_weight(2, 5)
    inbox[r] = outbox[r]

    with jax.named_scope("in2"):
        for i in range(3, 5):
            for part in range(2):
                load(i, part).wait()
        for copy in small_local:
            copy.wait()
        for copy in small_in:
            copy.wait_recv()
        heads_held = half // breadth
        for h in range(cores * heads_held):
            reward_row[:, pl.ds(h * breadth, breadth)] = rewards[
                h // heads_held, pl.ds(h % heads_held, 1), :
            ]
    with jax.named_scope("within0"):
        lax.fori_loop(0, members // 2, within, 0)

    def wait_states(i, c):
        j = flip(r, i, members)
        copy = member_copy(outbox, inbox, j, j, s_send, s_recv)
        copy.wait_recv()
        copy.wait_send()
        return c

    with jax.named_scope("wait_states"):
        lax.fori_loop(1, members, wait_states, 0)

    upper, lower = pl.ds(0, breadth), pl.ds(breadth, breadth)

    def advance(box, state):
        s0, s1, d0, d1 = state
        e0, e1 = unpack_rows(box[pl.ds(2 * breadth, EXTRA), :])
        return (
            s0 * e0 + box[upper, :].astype(F32), s1 * e1 + box[lower, :].astype(F32),
            d0 * e0, d1 * e1,
        )

    def scan(j, state):
        before[j, upper, :] = state[0]
        before[j, lower, :] = state[1]
        before_dec[j, :, pl.ds(0, LANES)] = state[2]
        before_dec[j, :, pl.ds(LANES, LANES)] = state[3]
        return advance(inbox.at[j], state)

    zero, one = jnp.zeros((breadth, LANES), F32), jnp.ones((1, LANES), F32)
    with jax.named_scope("scan"):
        s0, s1, d0, d1 = lax.fori_loop(0, members, scan, (zero, zero, one, one))
        gout[upper, :] = s0.astype(BF16)
        gout[lower, :] = s1.astype(BF16)
        gout[pl.ds(2 * breadth, EXTRA), :] = pack_rows(jnp.concatenate([d0, d1], axis=1))

    def group_copy(g, slot):
        return pltpu.make_async_remote_copy(
            src_ref=gout, dst_ref=gin.at[slot], send_sem=g_send.at[g], recv_sem=g_recv.at[slot],
            device_id=above(g), device_id_type=MESH,
        )

    def send_group(g, c):
        group_copy(g, group).start()
        return c

    with jax.named_scope("send_group"):
        @pl.when(group < groups - 1)
        def _():
            pl.semaphore_wait(ready, groups - 1 - group)

        lax.fori_loop(group + 1, groups, send_group, 0)
        send_weight(5, 7)
    with jax.named_scope("within1"):
        lax.fori_loop(members // 2, 3 * members // 4, within, 0)

    def take_group(g, state):
        group_copy(g, g).wait_recv()
        return advance(gin.at[g], state)

    with jax.named_scope("take_group"):
        e0, e1, _, _ = lax.fori_loop(0, group, take_group, (zero, zero, one, one))

    def send_carry(step, c):
        i = members - 1 - step
        j = flip(r, i, members)
        d = before_dec[j]
        cbox[j, upper, :] = (e0 * d[:, :LANES] + before[j, upper, :]).astype(BF16)
        cbox[j, lower, :] = (e1 * d[:, LANES:] + before[j, lower, :]).astype(BF16)

        @pl.when(i > 0)
        def _():
            member_copy(cbox, carry, j, r, c_send, c_recv).start()

        return c

    with jax.named_scope("send_carry"):
        lax.fori_loop(0, members, send_carry, 0)
        carry[r] = cbox[r]
        send_weight(7, chunks)
    with jax.named_scope("within2"):
        lax.fori_loop(3 * members // 4, members, within, 0)

    def finish(i, c):
        q = flip(r, i, members)

        @pl.when(i > 0)
        def _():
            member_copy(cbox, carry, q, q, c_send, c_recv).wait_recv()

        lanes = pl.ds(pl.multiple_of(q * QUAD, QUAD), QUAD)
        a = split_heads(carry[q, upper, :], low_s)
        b = split_heads(carry[q, lower, :], low_s)
        none = jnp.zeros_like(a)
        state = jnp.concatenate(
            [jnp.concatenate([a, none], axis=1), jnp.concatenate([none, b], axis=1)], axis=0
        )
        for k in range(blocks):
            at = pl.ds(k * BLOCK, BLOCK)
            o = local_out[at, lanes] + dot_nt(recs[at, lanes], state)
            var = dot((o * o).astype(BF16), means)
            gated[at, lanes] = (o * lax.rsqrt(var + EPS) * swish[at, lanes]).astype(BF16)
        return c

    with jax.named_scope("finish"):
        lax.fori_loop(0, members, finish, 0)

    def project(k, c):
        weight_local(k).wait()
        weight_remote(k, other).wait_recv()
        total = dot(gated[:, pl.ds(0, half)], weight[0, k])
        for side in range(1, cores):
            total = total + dot(gated[:, pl.ds(side * half, half)], weight[side, k])
        out_ref[:, pl.ds(pl.multiple_of(k * CHUNK, CHUNK), CHUNK)] = total.astype(BF16)
        return c

    with jax.named_scope("project"):
        lax.fori_loop(0, chunks, project, 0)

    def drain_members(i, c):
        j = flip(r, i, members)
        member_copy(cbox, carry, j, j, c_send, c_recv).wait_send()
        return c

    def drain_groups(g, c):
        group_copy(g, group).wait_send()
        return c

    with jax.named_scope("drain"):
        lax.fori_loop(1, members, drain_members, 0)
        lax.fori_loop(group + 1, groups, drain_groups, 0)
        for k in range(chunks):
            weight_remote(k, core).wait_send()
        for copy in small_remote:
            copy.wait_send()


def shards(n, cores, rec, key, val, fade, gate, reward, gain, mapping):
    tokens, width = rec.shape
    breadth = reward.shape[1]
    half, depth = mapping.shape
    blocks, quads, chunks = tokens // BLOCK, width // QUAD, depth // CHUNK
    groups = n * cores // quads
    boxed = 2 * breadth + EXTRA
    dma = pltpu.SemaphoreType.DMA
    held = pltpu.VMEM((tokens, width), BF16)
    wide = pltpu.VMEM((tokens, width), F32)
    anywhere = pl.BlockSpec(memory_space=pl.ANY)
    return pl.pallas_call(
        functools.partial(kernel, n, cores, breadth),
        out_shape=pltpu.VMEM((tokens, depth), BF16),
        in_specs=[anywhere] * 8,
        out_specs=pl.BlockSpec(memory_space=pltpu.VMEM),
        scratch_shapes=[
            held, held, held, held, held,
            pltpu.VMEM((cores,) + reward.shape, F32),
            pltpu.VMEM((cores, 1, half), F32),
            pltpu.VMEM((cores, chunks, half, CHUNK), BF16),
            pltpu.VMEM((1, width), F32),
            wide, held, held, held, wide, wide,
            pltpu.VMEM((max(blocks - 1, 1), 2 * quads, breadth, LANES), BF16),
            pltpu.VMEM((blocks, 1, width), F32),
            pltpu.VMEM((blocks, 1, width), F32),
            pltpu.VMEM((quads, boxed, LANES), BF16),
            pltpu.VMEM((quads, boxed, LANES), BF16),
            pltpu.VMEM((quads, 2 * breadth, LANES), F32),
            pltpu.VMEM((quads, 1, QUAD), F32),
            pltpu.VMEM((boxed, LANES), BF16),
            pltpu.VMEM((groups, boxed, LANES), BF16),
            pltpu.VMEM((quads, 2 * breadth, LANES), BF16),
            pltpu.VMEM((quads, 2 * breadth, LANES), BF16),
            held,
            dma((10,)), dma((2,)), dma((2,)), dma((2,)),
            dma((chunks,)), dma((chunks,)), dma((chunks,)),
            dma((quads,)), dma((quads,)), dma((groups,)), dma((groups,)), dma((quads,)), dma((quads,)),
            pltpu.SemaphoreType.REGULAR,
        ],
        compiler_params=pltpu.CompilerParams(
            collective_id=0, has_side_effects=True, vmem_limit_bytes=52 * 2**20
        ),
    )(rec, key, val, fade, gate, reward, gain.reshape(1, -1), mapping)


def solution(mesh):
    tokens = P(("seq", "head"), None)
    placed = (tokens,) * 5 + (P("head", None), P("head"), P("head", None))
    return jax.shard_map(
        functools.partial(shards, mesh.shape["seq"], mesh.shape["head"]),
        mesh=mesh, in_specs=placed, out_specs=tokens, check_vma=False,
    )
```

time: 46.1 us -> 30.9 us (0.67)
  the two profiles are of different devices: /device:TPU:0 before, /device:TPU:24 now
where the time goes in v1:
time: 30.9 us; the launch traced here: 30.8 us
  Pallas kernels  29.5 us (95%)
  local copies, waits for them, and re-layouts  1.32 us (4%)
    pallas_call x1, Pallas kernels, shards(): pl.pallas_call(functools.partial(kernel, n, cores, breadth), out_shape=pl...  29.5 us
    unnamed x1, local copies, waits for them, and re-layouts  1.32 us

profile of v1, /device:TPU:24, one launch (start us, length us, event | category | flops | bytes accessed | tf_op | source)
XLA Modules:
  0.0 30.8 jit_solution(6884244131706706677)
XLA Ops:
  0.0 29.5 %shard_map.82 = bf16[256,4096]{1,0:T(8,128)(2,1)S(1)} custom-call(bf16[256,2048]{1,0:T(8,128)(2,1)} %rec_hbm.1, bf16[256,2048]{1,0:T(8,128)(2,1)} %key_hbm.1, bf16[256,2048]{1,0:T(8,128)(2,1)} %val_hbm.1, bf16[256,2048]{1,0:T(8,128)(2,1)} %fade_hbm.1, bf16[256,2048]{1,0:T(8,128)(2,1)} %gate_hbm.1, f32[16,64]{1,0:T(8,128)} %reward_hbm.1, f32[1,1024]{1,0:T(1,128)} %bitcast.1, ...), custom_call_target="tpu_custom_call" | custom-call | tf_op jit(solution)/shard_map/pallas_call | solution.py:434
  29.5 1.3 %copy.10 = bf16[256,4096]{1,0:T(8,128)(2,1)} copy(bf16[256,4096]{1,0:T(8,128)(2,1)S(1)} %shard_map.82) | data formatting | bytes 4194304

commit v2 on v1

--- a/solution.py
+++ b/solution.py
@@ -178,76 +178,131 @@
             device_id=place(j), device_id_type=MESH,
         )
 
-    def decays(step, c):
-        i = members - 1 - step
-        q = flip(r, i, members)
-        lanes = pl.ds(pl.multiple_of(q * QUAD, QUAD), QUAD)
-        states = [jnp.zeros((breadth, LANES), F32) for _ in range(2)]
-        pref = jnp.zeros((1, QUAD), F32)
-        for b in range(blocks):
-            at = pl.ds(b * BLOCK, BLOCK)
+    def quad_lanes(q):
+        return pl.ds(pl.multiple_of(q * QUAD, QUAD), QUAD)
+
+    def decays(qs):
+        cells = [(k, b) for k in range(len(qs)) for b in range(blocks)]
+        cums, logs, vbs, kms = {}, {}, {}, {}
+        for k, b in cells:
+            at, lanes = pl.ds(b * BLOCK, BLOCK), quad_lanes(qs[k])
             log_decay = -jnp.exp(fade[at, lanes].astype(F32))
             hi = log_decay.astype(BF16)
             lo = (log_decay - hi.astype(F32)).astype(BF16)
             cum = dot(incl, jnp.concatenate([hi, lo], axis=0))
-            mid, total = cum[BLOCK // 2 - 1 : BLOCK // 2], cum[BLOCK - 1 :]
-            km = (key[at, lanes].astype(F32) * jnp.exp(mid - cum)).astype(BF16)
-            vb = dot(val[at, lanes], centre).astype(BF16)
             cumx[at, lanes] = cum - log_decay
-            key_mid[at, lanes] = km
-            centred[at, lanes] = vb
-            pref_row[b, :, lanes] = pref
+            cums[k, b] = cum
+        for k, b in cells:
+            at, lanes = pl.ds(b * BLOCK, BLOCK), quad_lanes(qs[k])
+            vbs[k, b] = dot(val[at, lanes], centre).astype(BF16)
+            centred[at, lanes] = vbs[k, b]
+        for k, b in cells:
+            at, lanes = pl.ds(b * BLOCK, BLOCK), quad_lanes(qs[k])
+            cum = cums[k, b]
+            mid = cum[BLOCK // 2 - 1 : BLOCK // 2]
+            kms[k, b] = (key[at, lanes].astype(F32) * jnp.exp(mid - cum)).astype(BF16)
+            key_mid[at, lanes] = kms[k, b]
             mid_row[b, :, lanes] = mid
-            end, whole, begin = jnp.exp(total - mid), jnp.exp(total), jnp.exp(mid)
+        products = {}
+        for k, b in cells:
             for j in range(2):
                 cut = slice(j * LANES, (j + 1) * LANES)
-                if b > 0:
-                    entering[b - 1, 2 * q + j] = (states[j] * begin[:, cut]).astype(BF16)
-                product = dot_tn(vb[:, cut], km[:, cut])
-                own = jnp.where(low_s, product[:breadth], product[breadth:])
-                states[j] = states[j] * whole[:, cut] + own * end[:, cut]
-            pref = pref + total
-        for j in range(2):
-            outbox[q, pl.ds(j * breadth, breadth), :] = states[j].astype(BF16)
-        outbox[q, pl.ds(2 * breadth, EXTRA), :] = pack_rows(jnp.exp(pref))
-
-        @pl.when(i > 0)
-        def _():
-            member_copy(outbox, inbox, q, r, s_send, s_recv).start()
-
-        return c
-
-    def within(step, c):
-        q = flip(r, step, members)
-        lanes = pl.ds(pl.multiple_of(q * QUAD, QUAD), QUAD)
-        gain = gains[q // span, :, pl.ds(pl.multiple_of((q % span) * QUAD, QUAD), QUAD)]
-        reward = reward_row[:, lanes]
-        for b in range(blocks):
-            at = pl.ds(b * BLOCK, BLOCK)
+                products[k, b, j] = dot_tn(vbs[k, b][:, cut], kms[k, b][:, cut])
+        for k, q in enumerate(qs):
+            lanes = quad_lanes(q)
+            states = [jnp.zeros((breadth, LANES), F32) for _ in range(2)]
+            pref = jnp.zeros((1, QUAD), F32)
+            for b in range(blocks):
+                cum = cums[k, b]
+                mid, total = cum[BLOCK // 2 - 1 : BLOCK // 2], cum[BLOCK - 1 :]
+                end, whole, begin = jnp.exp(total - mid), jnp.exp(total), jnp.exp(mid)
+                pref_row[b, :, lanes] = pref
+                for j in range(2):
+                    cut = slice(j * LANES, (j + 1) * LANES)
+                    if b > 0:
+                        entering[b - 1, 2 * q + j] = (states[j] * begin[:, cut]).astype(BF16)
+                    product = products[k, b, j]
+                    own = jnp.where(low_s, product[:breadth], product[breadth:])
+                    states[j] = states[j] * whole[:, cut] + own * end[:, cut]
+                pref = pref + total
+            for j in range(2):
+                outbox[q, pl.ds(j * breadth, breadth), :] = states[j].astype(BF16)
+            outbox[q, pl.ds(2 * breadth, EXTRA), :] = pack_rows(jnp.exp(pref))
+
+    def within(qs):
+        cells = [(k, b) for k in range(len(qs)) for b in range(blocks)]
+        rms, diags, scored = {}, {}, {}
+        for k, b in cells:
+            q = qs[k]
+            at, lanes = pl.ds(b * BLOCK, BLOCK), quad_lanes(q)
+            cx = cumx[at, lanes]
+            rf = rec[at, lanes].astype(F32)
+            rms[k, b] = (rf * jnp.exp(cx - mid_row[b, :, lanes])).astype(BF16)
+            recs[at, lanes] = (rf * jnp.exp(cx + pref_row[b, :, lanes])).astype(BF16)
+            own = rf * key[at, lanes].astype(F32) * reward_row[:, lanes]
+            diags[k, b] = dot(own.astype(BF16), ones)
+            kb = key_mid[at, lanes]
+            for j in range(2):
+                cut = slice(j * LANES, (j + 1) * LANES)
+                scored[k, b, j] = dot_nt(rms[k, b][:, cut], split_heads(kb[:, cut], low))
+        for k, b in cells:
+            q = qs[k]
+            at, lanes = pl.ds(b * BLOCK, BLOCK), quad_lanes(q)
+            gain = gains[q // span, :, pl.ds(pl.multiple_of((q % span) * QUAD, QUAD), QUAD)]
             g = gate[at, lanes].astype(F32)
             swish[at, lanes] = g / (1.0 + jnp.exp(-g)) * gain
-            cx = cumx[at, lanes]
-            rf = rec[at, lanes].astype(F32)
-            kb, vb = key_mid[at, lanes], centred[at, lanes]
-            rm = (rf * jnp.exp(cx - mid_row[b, :, lanes])).astype(BF16)
-            recs[at, lanes] = (rf * jnp.exp(cx + pref_row[b, :, lanes])).astype(BF16)
-            own = rf * key[at, lanes].astype(F32) * reward
-            diag = dot(own.astype(BF16), ones)
+        for k, b in cells:
+            q = qs[k]
+            at, lanes = pl.ds(b * BLOCK, BLOCK), quad_lanes(q)
+            vb = centred[at, lanes]
             for j in range(2):
                 cut = slice(j * LANES, (j + 1) * LANES)
-                scores = dot_nt(rm[:, cut], split_heads(kb[:, cut], low))
-                scores = jnp.where(t_id > s_id, scores, 0.0).astype(BF16)
-                o = dot(scores, split_heads(vb[:, cut], low)) + diag[:, cut] * vb[:, cut].astype(F32)
+                scores = jnp.where(t_id > s_id, scored[k, b, j], 0.0).astype(BF16)
+                o = dot(scores, split_heads(vb[:, cut], low))
                 if b > 0:
-                    o = o + dot_nt(rm[:, cut], split_heads(entering[b - 1, 2 * q + j], low_s))
+                    o = o + dot_nt(rms[k, b][:, cut], split_heads(entering[b - 1, 2 * q + j], low_s))
+                o = o + diags[k, b][:, cut] * vb[:, cut].astype(F32)
                 local_out[at, pl.ds(pl.multiple_of(q * QUAD + j * LANES, LANES), LANES)] = o
-        return c
+
+    def withins(first, batch):
+        def body(step, c):
+            within([flip(r, first + step * batch + k, members) for k in range(batch)])
+            return c
+        return body
+
+    def finish(qs):
+        cells = [(k, b) for k in range(len(qs)) for b in range(blocks)]
+        states, outs, variances = [], {}, {}
+        for q in qs:
+            a = split_heads(carry[q, upper, :], low_s)
+            b = split_heads(carry[q, lower, :], low_s)
+            none = jnp.zeros_like(a)
+            states.append(jnp.concatenate(
+                [jnp.concatenate([a, none], axis=1), jnp.concatenate([none, b], axis=1)], axis=0
+            ))
+        for k, b in cells:
+            at, lanes = pl.ds(b * BLOCK, BLOCK), quad_lanes(qs[k])
+            outs[k, b] = local_out[at, lanes] + dot_nt(recs[at, lanes], states[k])
+        for k, b in cells:
+            variances[k, b] = dot((outs[k, b] * outs[k, b]).astype(BF16), means)
+        for k, b in cells:
+            at, lanes = pl.ds(b * BLOCK, BLOCK), quad_lanes(qs[k])
+            scale = lax.rsqrt(variances[k, b] + EPS) * swish[at, lanes]
+            gated[at, lanes] = (outs[k, b] * scale).astype(BF16)
+
+    upper, lower = pl.ds(0, breadth), pl.ds(breadth, breadth)
+    far = [flip(r, i, members) for i in range(members - 1, members // 2 - 1, -1)]
+    near = [flip(r, i, members) for i in range(members // 2 - 1, -1, -1)]
 
     with jax.named_scope("in0"):
         for i in range(3):
             load(i, 0).wait()
+    with jax.named_scope("decays0"):
+        decays(far)
     with jax.named_scope("barrier"):
         pl.semaphore_wait(barrier, members - 1 + group)
+        for q in far:
+            member_copy(outbox, inbox, q, r, s_send, s_recv).start()
         for copy in small_remote:
             copy.start()
 
@@ -256,17 +311,16 @@
             return c
 
         lax.fori_loop(0, group, here, 0)
-        send_weight(0, 2)
-        for k in range(chunks):
-            weight_local(k).start()
-    with jax.named_scope("decays0"):
-        lax.fori_loop(0, members // 2, decays, 0)
     with jax.named_scope("in1"):
         for i in range(3):
             load(i, 1).wait()
+        for k in range(chunks):
+            weight_local(k).start()
     with jax.named_scope("decays1"):
-        lax.fori_loop(members // 2, members, decays, 0)
-    send_weight(2, 5)
+        decays(near)
+    for q in near[:-1]:
+        member_copy(outbox, inbox, q, r, s_send, s_recv).start()
+    send_weight(0, 3)
     inbox[r] = outbox[r]
 
     with jax.named_scope("in2"):
@@ -283,7 +337,7 @@
                 h // heads_held, pl.ds(h % heads_held, 1), :
             ]
     with jax.named_scope("within0"):
-        lax.fori_loop(0, members // 2, within, 0)
+        lax.fori_loop(0, 2, withins(0, 2), 0)
 
     def wait_states(i, c):
         j = flip(r, i, members)
@@ -294,8 +348,6 @@
 
     with jax.named_scope("wait_states"):
         lax.fori_loop(1, members, wait_states, 0)
-
-    upper, lower = pl.ds(0, breadth), pl.ds(breadth, breadth)
 
     def advance(box, state):
         s0, s1, d0, d1 = state
@@ -335,9 +387,9 @@
             pl.semaphore_wait(ready, groups - 1 - group)
 
         lax.fori_loop(group + 1, groups, send_group, 0)
-        send_weight(5, 7)
+        send_weight(3, 5)
     with jax.named_scope("within1"):
-        lax.fori_loop(members // 2, 3 * members // 4, within, 0)
+        withins(members // 2, 2)(0, 0)
 
     def take_group(g, state):
         group_copy(g, g).wait_recv()
@@ -362,33 +414,17 @@
     with jax.named_scope("send_carry"):
         lax.fori_loop(0, members, send_carry, 0)
         carry[r] = cbox[r]
-        send_weight(7, chunks)
+        send_weight(5, chunks)
     with jax.named_scope("within2"):
-        lax.fori_loop(3 * members // 4, members, within, 0)
-
-    def finish(i, c):
-        q = flip(r, i, members)
-
-        @pl.when(i > 0)
-        def _():
-            member_copy(cbox, carry, q, q, c_send, c_recv).wait_recv()
-
-        lanes = pl.ds(pl.multiple_of(q * QUAD, QUAD), QUAD)
-        a = split_heads(carry[q, upper, :], low_s)
-        b = split_heads(carry[q, lower, :], low_s)
-        none = jnp.zeros_like(a)
-        state = jnp.concatenate(
-            [jnp.concatenate([a, none], axis=1), jnp.concatenate([none, b], axis=1)], axis=0
-        )
-        for k in range(blocks):
-            at = pl.ds(k * BLOCK, BLOCK)
-            o = local_out[at, lanes] + dot_nt(recs[at, lanes], state)
-            var = dot((o * o).astype(BF16), means)
-            gated[at, lanes] = (o * lax.rsqrt(var + EPS) * swish[at, lanes]).astype(BF16)
-        return c
-
-    with jax.named_scope("finish"):
-        lax.fori_loop(0, members, finish, 0)
+        withins(3 * members // 4, 2)(0, 0)
+
+    for name, qs in (("near", near), ("far", far)):
+        with jax.named_scope("wait_" + name):
+            for q in qs:
+                if q is not near[-1]:
+                    member_copy(cbox, carry, q, q, c_send, c_recv).wait_recv()
+        with jax.named_scope("finish_" + name):
+            finish(qs)
 
     def project(k, c):
         weight_local(k).wait()

time: 30.9 us -> 26.6 us (0.86)
  Pallas kernels: 29.5 us -> 25.1 us
    pallas_call x1, Pallas kernels: 29.5 us -> 25.1 us  [shards(): pl.pallas_call(functools.partial(kernel, n, cores, breadth), out_shape=pl...]
where the time goes in v2:
time: 26.6 us; the launch traced here: 26.4 us
  Pallas kernels  25.1 us (94%)
  local copies, waits for them, and re-layouts  1.32 us (5%)
    pallas_call x1, Pallas kernels, shards(): pl.pallas_call(functools.partial(kernel, n, cores, breadth), out_shape=pl...  25.1 us
    unnamed x1, local copies, waits for them, and re-layouts  1.32 us

profile of v2, /device:TPU:24, one launch (start us, length us, event | category | flops | bytes accessed | tf_op | source)
XLA Modules:
  0.0 26.4 jit_solution(9965241861674122875)
XLA Ops:
  0.0 25.1 %shard_map.82 = bf16[256,4096]{1,0:T(8,128)(2,1)S(1)} custom-call(bf16[256,2048]{1,0:T(8,128)(2,1)} %rec_hbm.1, bf16[256,2048]{1,0:T(8,128)(2,1)} %key_hbm.1, bf16[256,2048]{1,0:T(8,128)(2,1)} %val_hbm.1, bf16[256,2048]{1,0:T(8,128)(2,1)} %fade_hbm.1, bf16[256,2048]{1,0:T(8,128)(2,1)} %gate_hbm.1, f32[16,64]{1,0:T(8,128)} %reward_hbm.1, f32[1,1024]{1,0:T(1,128)} %bitcast.1, ...), custom_call_target="tpu_custom_call" | custom-call | tf_op jit(solution)/shard_map/pallas_call | solution.py:470
  25.1 1.3 %copy.10 = bf16[256,4096]{1,0:T(8,128)(2,1)} copy(bf16[256,4096]{1,0:T(8,128)(2,1)S(1)} %shard_map.82) | data formatting | bytes 4194304

commit v3 on v1

v3 whole, which is shorter than its diff:
```python
import functools

import jax
import jax.numpy as jnp
from jax import lax
from jax.experimental import pallas as pl
from jax.experimental.pallas import tpu as pltpu
from jax.sharding import PartitionSpec as P

BLOCK = 128
LANES = 128
QUAD = 256
CHUNK = 512
LEAD = 4
EXTRA = 8
EPS = 1e-05
MESH = pl.DeviceIdType.MESH
F32 = jnp.float32
BF16 = jnp.bfloat16


def dot(a, b):
    return jnp.dot(a, b, preferred_element_type=F32)


def dot_nt(a, b):
    return lax.dot_general(a, b, (((1,), (1,)), ((), ())), preferred_element_type=F32)


def dot_tn(a, b):
    return lax.dot_general(a, b, (((0,), (0,)), ((), ())), preferred_element_type=F32)


def split_heads(x, low):
    zero = jnp.zeros_like(x)
    return jnp.concatenate([jnp.where(low, x, zero), jnp.where(low, zero, x)], axis=0)


def flip(r, i, members):
    q, bit = 0, 1
    while bit < members:
        q = q + bit * (((r // bit) % 2 + (i // bit) % 2) % 2)
        bit *= 2
    return q


def kernel(
    n, cores, breadth,
    rec_hbm, key_hbm, val_hbm, fade_hbm, gate_hbm, reward_hbm, gain_hbm, map_hbm,
    out_ref,
    held, rewards, gains, weight,
    reward_row, cumx, key_mid, centred, recs, local_out, swish, entering, pref_row, mid_row,
    outbox, inbox, before, before_dec, gout, gin, cbox, carry, gated, partial,
    in_sem, p_local, p_send, p_recv, w_sem, w_send,
    s_send, s_recv, g_send, g_recv, c_send, c_recv, ready,
):
    me, core = lax.axis_index("seq"), lax.axis_index("head")
    other = 1 - core
    tokens, width = held.shape[1:]
    half = width // cores
    blocks, quads = tokens // BLOCK, half // QUAD
    chunks = weight.shape[1]
    lead = min(LEAD, chunks)
    members = half // LANES
    span = members // cores
    groups = n // span
    group = me // span
    r = (me % span) * cores + core
    peers = [flip(r, i, members) for i in range(members - 1, 0, -1)]
    fade, key, val, rec, gate = (held.at[i] for i in range(5))
    sources = (fade_hbm, key_hbm, val_hbm, rec_hbm, gate_hbm)

    def place(q):
        return (group * span + q // cores, q % cores)

    def above(g):
        return (g * span + me % span, core)

    barrier = pltpu.get_barrier_semaphore()
    for q in peers:
        pl.semaphore_signal(barrier, inc=1, device_id=place(q), device_id_type=MESH)

    for p in range(cores):
        for i in range(3):
            at = pl.ds(p * half, half)
            pltpu.make_async_copy(sources[i].at[:, at], held.at[i, :, at], in_sem.at[p]).start()

    def greet_above(g, c):
        pl.semaphore_signal(barrier, inc=1, device_id=above(g), device_id_type=MESH)
        return c

    lax.fori_loop(group + 1, groups, greet_above, 0)
    for i in range(3, 5):
        pltpu.make_async_copy(sources[i], held.at[i], in_sem.at[cores]).start()

    def wait_all(ref, sem):
        pltpu.make_async_copy(ref, ref, sem).wait()

    small = ((reward_hbm, rewards), (gain_hbm, gains))
    small_local = [
        pltpu.make_async_copy(src, dst.at[core], p_local.at[i]) for i, (src, dst) in enumerate(small)
    ]

    def small_copy(i, side):
        src, dst = small[i]
        return pltpu.make_async_remote_copy(
            src_ref=src, dst_ref=dst.at[side], send_sem=p_send.at[i], recv_sem=p_recv.at[i],
            device_id=(me, other), device_id_type=MESH,
        )

    for copy in small_local:
        copy.start()

    def columns(k):
        return map_hbm.at[:, pl.ds(k * CHUNK, CHUNK)]

    def weight_sem(k):
        return w_sem.at[max(k - lead + 1, 0)]

    def send_weight(start, stop):
        for k in range(start, min(stop, chunks)):
            pltpu.make_async_remote_copy(
                src_ref=columns(k), dst_ref=weight.at[core, k],
                send_sem=w_send.at[0], recv_sem=weight_sem(k),
                device_id=(me, other), device_id_type=MESH,
            ).start()

    t_id = lax.broadcasted_iota(jnp.int32, (BLOCK, 2 * BLOCK), 0)
    s_id = lax.rem(lax.broadcasted_iota(jnp.int32, (BLOCK, 2 * BLOCK), 1), BLOCK)
    incl = jnp.where(t_id >= s_id, 1.0, 0.0).astype(BF16)
    low = lax.broadcasted_iota(jnp.int32, (BLOCK, LANES), 1) < breadth
    low_s = lax.broadcasted_iota(jnp.int32, (breadth, LANES), 1) < breadth
    row_x = lax.broadcasted_iota(jnp.int32, (EXTRA, LANES), 0)
    head_i = lax.broadcasted_iota(jnp.int32, (QUAD, QUAD), 0)
    head_j = lax.broadcasted_iota(jnp.int32, (QUAD, QUAD), 1)
    same, equal = head_i // breadth == head_j // breadth, head_i == head_j
    means = jnp.where(same, 1.0 / breadth, 0.0).astype(BF16)
    centre = (jnp.where(equal, 1.0, 0.0) - jnp.where(same, 1.0 / breadth, 0.0)).astype(BF16)
    ones = jnp.where(same, 1.0, 0.0).astype(BF16)
    state_rows, decay_rows = pl.ds(0, breadth), pl.ds(breadth, EXTRA)
    cuts = [slice(j * LANES, (j + 1) * LANES) for j in range(2)]

    def pack_rows(dec):
        hi = dec.astype(BF16).astype(F32)
        return jnp.where(row_x == 0, hi, jnp.where(row_x == 1, dec - hi, 0.0)).astype(BF16)

    def unpack_rows(x):
        x = x.astype(F32)
        return x[0:1] + x[1:2]

    def quad_lanes(p, t):
        return pl.ds(p * half + t * QUAD, QUAD)

    def decays(p):
        cells = [(t, b) for t in range(quads) for b in range(blocks)]
        cums, vbs, kms, products = {}, {}, {}, {}
        for t, b in cells:
            at, lanes = pl.ds(b * BLOCK, BLOCK), quad_lanes(p, t)
            log_decay = -jnp.exp(fade[at, lanes].astype(F32))
            hi = log_decay.astype(BF16)
            lo = (log_decay - hi.astype(F32)).astype(BF16)
            cum = dot(incl, jnp.concatenate([hi, lo], axis=0))
            cumx[at, lanes] = cum - log_decay
            cums[t, b] = cum
        for t, b in cells:
            at, lanes = pl.ds(b * BLOCK, BLOCK), quad_lanes(p, t)
            vbs[t, b] = dot(val[at, lanes], centre).astype(BF16)
            centred[at, lanes] = vbs[t, b]
        for t, b in cells:
            at, lanes = pl.ds(b * BLOCK, BLOCK), quad_lanes(p, t)
            mid = cums[t, b][BLOCK // 2 - 1 : BLOCK // 2]
            kms[t, b] = (key[at, lanes].astype(F32) * jnp.exp(mid - cums[t, b])).astype(BF16)
            key_mid[at, lanes] = kms[t, b]
            mid_row[b, :, lanes] = mid
        for t, b in cells:
            for j, cut in enumerate(cuts):
                products[t, b, j] = dot_tn(vbs[t, b][:, cut], kms[t, b][:, cut])
        for t in range(quads):
            lanes = quad_lanes(p, t)
            states = [jnp.zeros((breadth, LANES), F32) for _ in range(2)]
            pref = jnp.zeros((1, QUAD), F32)
            for b in range(blocks):
                cum = cums[t, b]
                mid, total = cum[BLOCK // 2 - 1 : BLOCK // 2], cum[BLOCK - 1 :]
                end, whole, begin = jnp.exp(total - mid), jnp.exp(total), jnp.exp(mid)
                pref_row[b, :, lanes] = pref
                for j, cut in enumerate(cuts):
                    if b > 0:
                        entering[p, b - 1, 2 * t + j] = (states[j] * begin[:, cut]).astype(BF16)
                    product = products[t, b, j]
                    own = jnp.where(low_s, product[:breadth], product[breadth:])
                    states[j] = states[j] * whole[:, cut] + own * end[:, cut]
                pref = pref + total
            gone = jnp.exp(pref)
            for j, cut in enumerate(cuts):
                outbox[p, 2 * t + j, state_rows, :] = states[j].astype(BF16)
                outbox[p, 2 * t + j, decay_rows, :] = pack_rows(gone[:, cut])

    def within(units):
        cells = [(p, t, b) for p, t in units for b in range(blocks)]
        rms, diags, scored = {}, {}, {}
        for p, t, b in cells:
            at, lanes = pl.ds(b * BLOCK, BLOCK), quad_lanes(p, t)
            cx = cumx[at, lanes]
            rf = rec[at, lanes].astype(F32)
            rms[p, t, b] = (rf * jnp.exp(cx - mid_row[b, :, lanes])).astype(BF16)
            recs[at, lanes] = (rf * jnp.exp(cx + pref_row[b, :, lanes])).astype(BF16)
            own = rf * key[at, lanes].astype(F32) * reward_row[:, lanes]
            diags[p, t, b] = dot(own.astype(BF16), ones)
            kb = key_mid[at, lanes]
            for j, cut in enumerate(cuts):
                scored[p, t, b, j] = dot_nt(rms[p, t, b][:, cut], split_heads(kb[:, cut], low))
        for p, t, b in cells:
            at, lanes = pl.ds(b * BLOCK, BLOCK), quad_lanes(p, t)
            g = gate[at, lanes].astype(F32)
            swish[at, lanes] = g / (1.0 + jnp.exp(-g)) * gains[p, :, pl.ds(t * QUAD, QUAD)]
        for p, t, b in cells:
            at, lanes = pl.ds(b * BLOCK, BLOCK), quad_lanes(p, t)
            vb = centred[at, lanes]
            for j, cut in enumerate(cuts):
                scores = jnp.where(t_id > s_id, scored[p, t, b, j], 0.0).astype(BF16)
                o = dot(scores, split_heads(vb[:, cut], low))
                if b > 0:
                    came = split_heads(entering[p, b - 1, 2 * t + j], low_s)
                    o = o + dot_nt(rms[p, t, b][:, cut], came)
                o = o + diags[p, t, b][:, cut] * vb[:, cut].astype(F32)
                local_out[at, pl.ds(p * half + t * QUAD + j * LANES, LANES)] = o

    def finish(p):
        cells = [(t, b) for t in range(quads) for b in range(blocks)]
        states, outs, variances = [], {}, {}
        for t in range(quads):
            x, y = (split_heads(carry[p, 2 * t + j], low_s) for j in range(2))
            none = jnp.zeros_like(x)
            states.append(jnp.concatenate(
                [jnp.concatenate([x, none], axis=1), jnp.concatenate([none, y], axis=1)], axis=0
            ))
        for t, b in cells:
            at, lanes = pl.ds(b * BLOCK, BLOCK), quad_lanes(p, t)
            outs[t, b] = local_out[at, lanes] + dot_nt(recs[at, lanes], states[t])
        for t, b in cells:
            variances[t, b] = dot((outs[t, b] * outs[t, b]).astype(BF16), means)
        for t, b in cells:
            at, lanes = pl.ds(b * BLOCK, BLOCK), quad_lanes(p, t)
            scale = lax.rsqrt(variances[t, b] + EPS) * swish[at, lanes]
            gated[at, lanes] = (outs[t, b] * scale).astype(BF16)

    def member_copy(src, dst, p, j, send, recv):
        return pltpu.make_async_remote_copy(
            src_ref=src.at[p, j], dst_ref=dst.at[p, r], send_sem=send.at[p], recv_sem=recv.at[p],
            device_id=place(j), device_id_type=MESH,
        )

    def send_states(p):
        for q in peers:
            member_copy(outbox, inbox, p, q, s_send, s_recv).start()
        inbox[p, r] = outbox[p, r]

    some = pl.ds(0, members - 1)

    def advance(box, state):
        s, d = state
        e = unpack_rows(box[decay_rows, :])
        return s * e + box[state_rows, :].astype(F32), d * e

    nothing = (jnp.zeros((breadth, LANES), F32), jnp.ones((1, LANES), F32))

    def scan(p):
        state = nothing
        for j in range(members):
            before[p, j] = state[0]
            before_dec[p, j] = state[1]
            state = advance(inbox.at[p, j], state)
        gout[p, state_rows, :] = state[0].astype(BF16)
        gout[p, decay_rows, :] = pack_rows(state[1])

    def group_copy(p, g, slot):
        return pltpu.make_async_remote_copy(
            src_ref=gout.at[p], dst_ref=gin.at[p, slot],
            send_sem=g_send.at[p, g], recv_sem=g_recv.at[p, slot],
            device_id=above(g), device_id_type=MESH,
        )

    def send_group(p):
        def body(i, c):
            group_copy(p, groups - 1 - i, group).start()
            return c

        lax.fori_loop(0, groups - 1 - group, body, 0)

    def take_group(p):
        def body(g, state):
            group_copy(p, g, g).wait_recv()
            return advance(gin.at[p, g], state)

        return lax.fori_loop(0, group, body, nothing)[0]

    def send_carry(p, came):
        for j in range(members):
            cbox[p, j] = (came * before_dec[p, j] + before[p, j]).astype(BF16)
        for q in peers:
            member_copy(cbox, carry, p, q, c_send, c_recv).start()
        carry[p, r] = cbox[p, r]

    with jax.named_scope("in0"):
        wait_all(held.at[pl.ds(0, 3), :, pl.ds(0, half)], in_sem.at[0])
    with jax.named_scope("decays0"):
        decays(0)
    with jax.named_scope("barrier"):
        pl.semaphore_wait(barrier, members - 1 + group)
        send_states(0)
        for i in range(2):
            small_copy(i, core).start()

        def here(g, c):
            pl.semaphore_signal(ready, inc=1, device_id=above(g), device_id_type=MESH)
            return c

        lax.fori_loop(0, group, here, 0)
        for k in range(chunks):
            pltpu.make_async_copy(columns(k), weight.at[core, k], weight_sem(k)).start()
    for p in range(1, cores):
        with jax.named_scope("in1"):
            wait_all(held.at[pl.ds(0, 3), :, pl.ds(p * half, half)], in_sem.at[p])
        with jax.named_scope("decays1"):
            decays(p)
        with jax.named_scope("send1"):
            send_states(p)
    send_weight(0, 2)

    with jax.named_scope("in2"):
        wait_all(held.at[pl.ds(3, 2)], in_sem.at[cores])
        for i in range(2):
            small_local[i].wait()
            small_copy(i, other).wait_recv()
        for h in range(width // breadth):
            reward_row[:, pl.ds(h * breadth, breadth)] = rewards[
                h * breadth // half, pl.ds(h % (half // breadth), 1), :
            ]

    units = [(p, t) for p in range(cores) for t in range(quads)]
    done = 0

    def some_within(count):
        nonlocal done
        for at in range(done, min(done + count, len(units)), 2):
            with jax.named_scope("within"):
                within(units[at : at + 2])
        done += count

    some_within(4)
    for p in range(cores):
        with jax.named_scope("wait_states"):
            wait_all(inbox.at[p, some], s_recv.at[p])
        with jax.named_scope("scan"):
            scan(p)
        with jax.named_scope("send_group"):
            if p == 0:
                @pl.when(group < groups - 1)
                def _():
                    pl.semaphore_wait(ready, groups - 1 - group)

            send_group(p)

            @pl.when(group > 0)
            def _():
                send_weight(2 + p, 3 + p if p < cores - 1 else lead)

        some_within(2 if p < cores - 1 else len(units))
    for p in range(cores):
        with jax.named_scope("take_group"):
            came = take_group(p)
        with jax.named_scope("send_carry"):
            send_carry(p, came)
    with jax.named_scope("send_weight"):
        @pl.when(group == 0)
        def _():
            send_weight(2, lead)

        send_weight(lead, chunks)

    def project(k, first, last):
        at = pl.ds(k * CHUNK, CHUNK)
        total = partial[:, at] if first > 0 else None
        for p in range(first, last):
            term = dot(gated[:, pl.ds(p * half, half)], weight[p, k])
            total = term if total is None else total + term
        if last < cores:
            partial[:, at] = total
        else:
            out_ref[:, at] = total.astype(BF16)

    for p in range(cores - 1):
        with jax.named_scope("wait_carry"):
            wait_all(carry.at[p, some], c_recv.at[p])
        with jax.named_scope("finish"):
            finish(p)
    with jax.named_scope("wait_weight"):
        wait_all(weight.at[:, pl.ds(0, lead)], w_sem.at[0])
    with jax.named_scope("project_lead"):
        for k in range(lead):
            project(k, 0, cores - 1)
    with jax.named_scope("wait_carry"):
        wait_all(carry.at[cores - 1, some], c_recv.at[cores - 1])
    with jax.named_scope("finish"):
        finish(cores - 1)
    with jax.named_scope("project_led"):
        for k in range(lead):
            project(k, cores - 1, cores)
    for k in range(lead, chunks):
        with jax.named_scope("wait_weight"):
            wait_all(weight.at[:, k], weight_sem(k))
        with jax.named_scope("project_rest"):
            project(k, 0, cores)

    def drain_groups(g, c):
        for p in range(cores):
            group_copy(p, g, group).wait_send()
        return c

    with jax.named_scope("drain"):
        lax.fori_loop(group + 1, groups, drain_groups, 0)
        for p in range(cores):
            wait_all(outbox.at[p, some], s_send.at[p])
            wait_all(cbox.at[p, some], c_send.at[p])
        wait_all(weight.at[other], w_send.at[0])
        for i in range(2):
            small_copy(i, core).wait_send()


def shards(n, cores, rec, key, val, fade, gate, reward, gain, mapping):
    tokens, width = rec.shape
    breadth = reward.shape[1]
    half, depth = mapping.shape
    blocks, chunks, members = tokens // BLOCK, depth // CHUNK, half // LANES
    groups = n * cores // members
    boxed = breadth + EXTRA
    dma = pltpu.SemaphoreType.DMA
    narrow = pltpu.VMEM((tokens, width), BF16)
    wide = pltpu.VMEM((tokens, width), F32)
    return pl.pallas_call(
        functools.partial(kernel, n, cores, breadth),
        out_shape=pltpu.VMEM((tokens, depth), BF16),
        in_specs=[pl.BlockSpec(memory_space=pl.ANY)] * 8,
        out_specs=pl.BlockSpec(memory_space=pltpu.VMEM),
        scratch_shapes=[
            pltpu.VMEM((5, tokens, width), BF16),
            pltpu.VMEM((cores,) + reward.shape, F32),
            pltpu.VMEM((cores, 1, half), F32),
            pltpu.VMEM((cores, chunks, half, CHUNK), BF16),
            pltpu.VMEM((1, width), F32),
            wide, narrow, narrow, narrow, wide, wide,
            pltpu.VMEM((cores, max(blocks - 1, 1), members, breadth, LANES), BF16),
            pltpu.VMEM((blocks, 1, width), F32),
            pltpu.VMEM((blocks, 1, width), F32),
            pltpu.VMEM((cores, members, boxed, LANES), BF16),
            pltpu.VMEM((cores, members, boxed, LANES), BF16),
            pltpu.VMEM((cores, members, breadth, LANES), F32),
            pltpu.VMEM((cores, members, 1, LANES), F32),
            pltpu.VMEM((cores, boxed, LANES), BF16),
            pltpu.VMEM((cores, groups, boxed, LANES), BF16),
            pltpu.VMEM((cores, members, breadth, LANES), BF16),
            pltpu.VMEM((cores, members, breadth, LANES), BF16),
            narrow,
            pltpu.VMEM((tokens, depth), F32),
            dma((cores + 1,)), dma((2,)), dma((2,)), dma((2,)),
            dma((max(chunks - LEAD, 0) + 1,)), dma((1,)),
            dma((cores,)), dma((cores,)), dma((cores, groups)), dma((cores, groups)),
            dma((cores,)), dma((cores,)), pltpu.SemaphoreType.REGULAR,
        ],
        compiler_params=pltpu.CompilerParams(
            collective_id=0, has_side_effects=True, vmem_limit_bytes=52 * 2**20
        ),
    )(rec, key, val, fade, gate, reward, gain.reshape(1, -1), mapping)


def solution(mesh):
    tokens = P(("seq", "head"), None)
    placed = (tokens,) * 5 + (P("head", None), P("head"), P("head", None))
    return jax.shard_map(
        functools.partial(shards, mesh.shape["seq"], mesh.shape["head"]),
        mesh=mesh, in_specs=placed, out_specs=tokens, check_vma=False,
    )
```

time: 30.9 us -> 23.1 us (0.75)
  the two profiles are of different devices: /device:TPU:24 before, /device:TPU:17 now
where the time goes in v3:
time: 23.1 us; the launch traced here: 22.9 us
  Pallas kernels  21.5 us (93%)
  local copies, waits for them, and re-layouts  1.32 us (6%)
    pallas_call x1, Pallas kernels, shards(): pl.pallas_call(functools.partial(kernel, n, cores, breadth), out_shape=pl...  21.5 us
    unnamed x1, local copies, waits for them, and re-layouts  1.32 us

profile of v3, /device:TPU:17, one launch (start us, length us, event | category | flops | bytes accessed | tf_op | source)
XLA Modules:
  0.0 22.9 jit_solution(17241538955567965541)
XLA Ops:
  0.0 21.5 %shard_map.82 = bf16[256,4096]{1,0:T(8,128)(2,1)S(1)} custom-call(bf16[256,2048]{1,0:T(8,128)(2,1)} %rec_hbm.1, bf16[256,2048]{1,0:T(8,128)(2,1)} %key_hbm.1, bf16[256,2048]{1,0:T(8,128)(2,1)} %val_hbm.1, bf16[256,2048]{1,0:T(8,128)(2,1)} %fade_hbm.1, bf16[256,2048]{1,0:T(8,128)(2,1)} %gate_hbm.1, f32[16,64]{1,0:T(8,128)} %reward_hbm.1, f32[1,1024]{1,0:T(1,128)} %bitcast.1, ...), custom_call_target="tpu_custom_call" | custom-call | tf_op jit(solution)/shard_map/pallas_call | solution.py:441
  21.6 1.3 %copy.10 = bf16[256,4096]{1,0:T(8,128)(2,1)} copy(bf16[256,4096]{1,0:T(8,128)(2,1)S(1)} %shard_map.82) | data formatting | bytes 4194304

commit v4 on v3

--- a/solution.py
+++ b/solution.py
@@ -81,9 +81,10 @@
         pl.semaphore_signal(barrier, inc=1, device_id=place(q), device_id_type=MESH)
 
     for p in range(cores):
-        for i in range(3):
+        for i in (0, 2, 1):
             at = pl.ds(p * half, half)
-            pltpu.make_async_copy(sources[i].at[:, at], held.at[i, :, at], in_sem.at[p]).start()
+            sem = in_sem.at[i if p == 0 else p + 2]
+            pltpu.make_async_copy(sources[i].at[:, at], held.at[i, :, at], sem).start()
 
     def greet_above(g, c):
         pl.semaphore_signal(barrier, inc=1, device_id=above(g), device_id_type=MESH)
@@ -91,7 +92,7 @@
 
     lax.fori_loop(group + 1, groups, greet_above, 0)
     for i in range(3, 5):
-        pltpu.make_async_copy(sources[i], held.at[i], in_sem.at[cores]).start()
+        pltpu.make_async_copy(sources[i], held.at[i], in_sem.at[cores + 2]).start()
 
     def wait_all(ref, sem):
         pltpu.make_async_copy(ref, ref, sem).wait()
@@ -117,10 +118,11 @@
     def weight_sem(k):
         return w_sem.at[max(k - lead + 1, 0)]
 
-    def send_weight(start, stop):
-        for k in range(start, min(stop, chunks)):
+    def send_weight(start, stop=2 * chunks):
+        for piece in range(start, min(stop, 2 * chunks)):
+            k, rows = piece // 2, pl.ds(piece % 2 * (half // 2), half // 2)
             pltpu.make_async_remote_copy(
-                src_ref=columns(k), dst_ref=weight.at[core, k],
+                src_ref=map_hbm.at[rows, pl.ds(k * CHUNK, CHUNK)], dst_ref=weight.at[core, k, rows],
                 send_sem=w_send.at[0], recv_sem=weight_sem(k),
                 device_id=(me, other), device_id_type=MESH,
             ).start()
@@ -151,9 +153,14 @@
     def quad_lanes(p, t):
         return pl.ds(p * half + t * QUAD, QUAD)
 
+    def arrive(p, i):
+        if p == 0:
+            wait_all(held.at[i, :, pl.ds(0, half)], in_sem.at[i])
+
     def decays(p):
         cells = [(t, b) for t in range(quads) for b in range(blocks)]
         cums, vbs, kms, products = {}, {}, {}, {}
+        arrive(p, 0)
         for t, b in cells:
             at, lanes = pl.ds(b * BLOCK, BLOCK), quad_lanes(p, t)
             log_decay = -jnp.exp(fade[at, lanes].astype(F32))
@@ -162,10 +169,12 @@
             cum = dot(incl, jnp.concatenate([hi, lo], axis=0))
             cumx[at, lanes] = cum - log_decay
             cums[t, b] = cum
+        arrive(p, 2)
         for t, b in cells:
             at, lanes = pl.ds(b * BLOCK, BLOCK), quad_lanes(p, t)
             vbs[t, b] = dot(val[at, lanes], centre).astype(BF16)
             centred[at, lanes] = vbs[t, b]
+        arrive(p, 1)
         for t, b in cells:
             at, lanes = pl.ds(b * BLOCK, BLOCK), quad_lanes(p, t)
             mid = cums[t, b][BLOCK // 2 - 1 : BLOCK // 2]
@@ -226,7 +235,7 @@
                 o = o + diags[p, t, b][:, cut] * vb[:, cut].astype(F32)
                 local_out[at, pl.ds(p * half + t * QUAD + j * LANES, LANES)] = o
 
-    def finish(p):
+    def finish(p, between=()):
         cells = [(t, b) for t in range(quads) for b in range(blocks)]
         states, outs, variances = [], {}, {}
         for t in range(quads):
@@ -240,6 +249,8 @@
             outs[t, b] = local_out[at, lanes] + dot_nt(recs[at, lanes], states[t])
         for t, b in cells:
             variances[t, b] = dot((outs[t, b] * outs[t, b]).astype(BF16), means)
+        for k in between:
+            project(k, 0, p)
         for t, b in cells:
             at, lanes = pl.ds(b * BLOCK, BLOCK), quad_lanes(p, t)
             scale = lax.rsqrt(variances[t, b] + EPS) * swish[at, lanes]
@@ -302,8 +313,6 @@
             member_copy(cbox, carry, p, q, c_send, c_recv).start()
         carry[p, r] = cbox[p, r]
 
-    with jax.named_scope("in0"):
-        wait_all(held.at[pl.ds(0, 3), :, pl.ds(0, half)], in_sem.at[0])
     with jax.named_scope("decays0"):
         decays(0)
     with jax.named_scope("barrier"):
@@ -321,15 +330,19 @@
             pltpu.make_async_copy(columns(k), weight.at[core, k], weight_sem(k)).start()
     for p in range(1, cores):
         with jax.named_scope("in1"):
-            wait_all(held.at[pl.ds(0, 3), :, pl.ds(p * half, half)], in_sem.at[p])
+            wait_all(held.at[pl.ds(0, 3), :, pl.ds(p * half, half)], in_sem.at[p + 2])
         with jax.named_scope("decays1"):
             decays(p)
         with jax.named_scope("send1"):
             send_states(p)
-    send_weight(0, 2)
+    send_weight(0, 4)
+
+    @pl.when(group == 0)
+    def _():
+        send_weight(4, 5)
 
     with jax.named_scope("in2"):
-        wait_all(held.at[pl.ds(3, 2)], in_sem.at[cores])
+        wait_all(held.at[pl.ds(3, 2)], in_sem.at[cores + 2])
         for i in range(2):
             small_local[i].wait()
             small_copy(i, other).wait_recv()
@@ -362,22 +375,25 @@
 
             send_group(p)
 
+            @pl.when(group == 0)
+            def _():
+                send_carry(p, nothing[0])
+                if p < cores - 1:
+                    send_weight(5 + 2 * p, 7 + 2 * p)
+                else:
+                    send_weight(3 + 2 * cores)
+
             @pl.when(group > 0)
             def _():
-                send_weight(2 + p, 3 + p if p < cores - 1 else lead)
+                send_weight(4 + 2 * p, 6 + 2 * p)
 
         some_within(2 if p < cores - 1 else len(units))
-    for p in range(cores):
-        with jax.named_scope("take_group"):
-            came = take_group(p)
-        with jax.named_scope("send_carry"):
-            send_carry(p, came)
-    with jax.named_scope("send_weight"):
-        @pl.when(group == 0)
+    with jax.named_scope("take_group"):
+        @pl.when(group > 0)
         def _():
-            send_weight(2, lead)
-
-        send_weight(lead, chunks)
+            for p in range(cores):
+                send_carry(p, take_group(p))
+            send_weight(4 + 2 * cores)
 
     def project(k, first, last):
         at = pl.ds(k * CHUNK, CHUNK)
@@ -398,19 +414,20 @@
     with jax.named_scope("wait_weight"):
         wait_all(weight.at[:, pl.ds(0, lead)], w_sem.at[0])
     with jax.named_scope("project_lead"):
-        for k in range(lead):
+        for k in range(lead - 2):
             project(k, 0, cores - 1)
     with jax.named_scope("wait_carry"):
         wait_all(carry.at[cores - 1, some], c_recv.at[cores - 1])
     with jax.named_scope("finish"):
-        finish(cores - 1)
+        finish(cores - 1, range(lead - 2, lead))
     with jax.named_scope("project_led"):
         for k in range(lead):
             project(k, cores - 1, cores)
-    for k in range(lead, chunks):
-        with jax.named_scope("wait_weight"):
+    with jax.named_scope("wait_weight"):
+        for k in range(lead, chunks):
             wait_all(weight.at[:, k], weight_sem(k))
-        with jax.named_scope("project_rest"):
+    with jax.named_scope("project_rest"):
+        for k in range(lead, chunks):
             project(k, 0, cores)
 
     def drain_groups(g, c):
@@ -463,7 +480,7 @@
             pltpu.VMEM((cores, members, breadth, LANES), BF16),
             narrow,
             pltpu.VMEM((tokens, depth), F32),
-            dma((cores + 1,)), dma((2,)), dma((2,)), dma((2,)),
+            dma((cores + 3,)), dma((2,)), dma((2,)), dma((2,)),
             dma((max(chunks - LEAD, 0) + 1,)), dma((1,)),
             dma((cores,)), dma((cores,)), dma((cores, groups)), dma((cores, groups)),
             dma((cores,)), dma((cores,)), pltpu.SemaphoreType.REGULAR,

time: 23.1 us -> 23.2 us (level)
  Pallas kernels: 21.5 us -> 21.8 us
where the time goes in v4:
time: 23.2 us; the launch traced here: 23.1 us
  Pallas kernels  21.8 us (94%)
  local copies, waits for them, and re-layouts  1.32 us (6%)
    pallas_call x1, Pallas kernels, shards(): pl.pallas_call(functools.partial(kernel, n, cores, breadth), out_shape=pl...  21.8 us
    unnamed x1, local copies, waits for them, and re-layouts  1.32 us

profile of v4, /device:TPU:17, one launch (start us, length us, event | category | flops | bytes accessed | tf_op | source)
XLA Modules:
  0.0 23.1 jit_solution(6491027295230098305)
XLA Ops:
  0.0 21.8 %shard_map.82 = bf16[256,4096]{1,0:T(8,128)(2,1)S(1)} custom-call(bf16[256,2048]{1,0:T(8,128)(2,1)} %rec_hbm.1, bf16[256,2048]{1,0:T(8,128)(2,1)} %key_hbm.1, bf16[256,2048]{1,0:T(8,128)(2,1)} %val_hbm.1, bf16[256,2048]{1,0:T(8,128)(2,1)} %fade_hbm.1, bf16[256,2048]{1,0:T(8,128)(2,1)} %gate_hbm.1, f32[16,64]{1,0:T(8,128)} %reward_hbm.1, f32[1,1024]{1,0:T(1,128)} %bitcast.1, ...), custom_call_target="tpu_custom_call" | custom-call | tf_op jit(solution)/shard_map/pallas_call | solution.py:458
  21.8 1.3 %copy.10 = bf16[256,4096]{1,0:T(8,128)(2,1)} copy(bf16[256,4096]{1,0:T(8,128)(2,1)S(1)} %shard_map.82) | data formatting | bytes 4194304

commit v5 on v4

--- a/solution.py
+++ b/solution.py
@@ -12,6 +12,7 @@
 QUAD = 256
 CHUNK = 512
 LEAD = 4
+WAYS = 2
 EXTRA = 8
 EPS = 1e-05
 MESH = pl.DeviceIdType.MESH
@@ -58,15 +59,19 @@
     other = 1 - core
     tokens, width = held.shape[1:]
     half = width // cores
-    blocks, quads = tokens // BLOCK, half // QUAD
+    parts, span = outbox.shape[:2]
+    ways = parts // cores
+    lane = width // parts
+    blocks, quads = tokens // BLOCK, lane // QUAD
     chunks = weight.shape[1]
     lead = min(LEAD, chunks)
-    members = half // LANES
-    span = members // cores
+    members = span * cores
     groups = n // span
     group = me // span
-    r = (me % span) * cores + core
+    chip = me % span
+    r = chip * cores + core
     peers = [flip(r, i, members) for i in range(members - 1, 0, -1)]
+    chips = [flip(chip, i, span) for i in range(span - 1, -1, -1)]
     fade, key, val, rec, gate = (held.at[i] for i in range(5))
     sources = (fade_hbm, key_hbm, val_hbm, rec_hbm, gate_hbm)
 
@@ -151,7 +156,7 @@
         return x[0:1] + x[1:2]
 
     def quad_lanes(p, t):
-        return pl.ds(p * half + t * QUAD, QUAD)
+        return pl.ds(p * lane + t * QUAD, QUAD)
 
     def arrive(p, i):
         if p == 0:
@@ -222,7 +227,7 @@
         for p, t, b in cells:
             at, lanes = pl.ds(b * BLOCK, BLOCK), quad_lanes(p, t)
             g = gate[at, lanes].astype(F32)
-            swish[at, lanes] = g / (1.0 + jnp.exp(-g)) * gains[p, :, pl.ds(t * QUAD, QUAD)]
+            swish[at, lanes] = g / (1.0 + jnp.exp(-g)) * gains[p * lane // half, :, pl.ds(p * lane % half + t * QUAD, QUAD)]
         for p, t, b in cells:
             at, lanes = pl.ds(b * BLOCK, BLOCK), quad_lanes(p, t)
             vb = centred[at, lanes]
@@ -233,39 +238,51 @@
                     came = split_heads(entering[p, b - 1, 2 * t + j], low_s)
                     o = o + dot_nt(rms[p, t, b][:, cut], came)
                 o = o + diags[p, t, b][:, cut] * vb[:, cut].astype(F32)
-                local_out[at, pl.ds(p * half + t * QUAD + j * LANES, LANES)] = o
-
-    def finish(p, between=()):
-        cells = [(t, b) for t in range(quads) for b in range(blocks)]
-        states, outs, variances = [], {}, {}
-        for t in range(quads):
-            x, y = (split_heads(carry[p, 2 * t + j], low_s) for j in range(2))
-            none = jnp.zeros_like(x)
-            states.append(jnp.concatenate(
-                [jnp.concatenate([x, none], axis=1), jnp.concatenate([none, y], axis=1)], axis=0
-            ))
-        for t, b in cells:
-            at, lanes = pl.ds(b * BLOCK, BLOCK), quad_lanes(p, t)
-            outs[t, b] = local_out[at, lanes] + dot_nt(recs[at, lanes], states[t])
-        for t, b in cells:
-            variances[t, b] = dot((outs[t, b] * outs[t, b]).astype(BF16), means)
+                local_out[at, pl.ds(p * lane + t * QUAD + j * LANES, LANES)] = o
+
+    def finish(ps, between=()):
+        cells = [(p, t, b) for p in ps for t in range(quads) for b in range(blocks)]
+        states, outs, variances = {}, {}, {}
+        for p in ps:
+            for t in range(quads):
+                x, y = (split_heads(carry[p, 2 * t + j], low_s) for j in range(2))
+                none = jnp.zeros_like(x)
+                states[p, t] = jnp.concatenate(
+                    [jnp.concatenate([x, none], axis=1), jnp.concatenate([none, y], axis=1)], axis=0
+                )
+        for p, t, b in cells:
+            at, lanes = pl.ds(b * BLOCK, BLOCK), quad_lanes(p, t)
+            outs[p, t, b] = local_out[at, lanes] + dot_nt(recs[at, lanes], states[p, t])
+        for p, t, b in cells:
+            out = outs[p, t, b]
+            variances[p, t, b] = dot((out * out).astype(BF16), means)
         for k in between:
-            project(k, 0, p)
-        for t, b in cells:
-            at, lanes = pl.ds(b * BLOCK, BLOCK), quad_lanes(p, t)
-            scale = lax.rsqrt(variances[t, b] + EPS) * swish[at, lanes]
-            gated[at, lanes] = (outs[t, b] * scale).astype(BF16)
-
-    def member_copy(src, dst, p, j, send, recv):
-        return pltpu.make_async_remote_copy(
-            src_ref=src.at[p, j], dst_ref=dst.at[p, r], send_sem=send.at[p], recv_sem=recv.at[p],
-            device_id=place(j), device_id_type=MESH,
-        )
+            project(k, 0, cores - 1)
+        for p, t, b in cells:
+            at, lanes = pl.ds(b * BLOCK, BLOCK), quad_lanes(p, t)
+            scale = lax.rsqrt(variances[p, t, b] + EPS) * swish[at, lanes]
+            gated[at, lanes] = (outs[p, t, b] * scale).astype(BF16)
 
     def send_states(p):
-        for q in peers:
-            member_copy(outbox, inbox, p, q, s_send, s_recv).start()
-        inbox[p, r] = outbox[p, r]
+        way, owner = p // cores, p % cores
+        for t in chips[:-1]:
+            pltpu.make_async_remote_copy(
+                src_ref=outbox.at[p, t], dst_ref=inbox.at[way, r],
+                send_sem=s_send.at[0], recv_sem=s_recv.at[way],
+                device_id=(group * span + t, owner), device_id_type=MESH,
+            ).start()
+
+        @pl.when(core == owner)
+        def _():
+            inbox[way, r] = outbox[p, chip]
+
+        @pl.when(core != owner)
+        def _():
+            pltpu.make_async_remote_copy(
+                src_ref=outbox.at[p, chip], dst_ref=inbox.at[way, r],
+                send_sem=s_send.at[0], recv_sem=s_recv.at[way],
+                device_id=(me, owner), device_id_type=MESH,
+            ).start()
 
     some = pl.ds(0, members - 1)
 
@@ -306,12 +323,26 @@
 
         return lax.fori_loop(0, group, body, nothing)[0]
 
-    def send_carry(p, came):
+    def send_carry(way, came):
+        p = way * cores + core
         for j in range(members):
-            cbox[p, j] = (came * before_dec[p, j] + before[p, j]).astype(BF16)
+            cbox[way, j] = (came * before_dec[way, j] + before[way, j]).astype(BF16)
         for q in peers:
-            member_copy(cbox, carry, p, q, c_send, c_recv).start()
-        carry[p, r] = cbox[p, r]
+            pltpu.make_async_remote_copy(
+                src_ref=cbox.at[way, q], dst_ref=carry.at[p, chip],
+                send_sem=c_send.at[0], recv_sem=c_recv.at[p],
+                device_id=place(q), device_id_type=MESH,
+            ).start()
+        carry[p, chip] = cbox[way, r]
+
+    def wait_carry(p):
+        @pl.when(core == p % cores)
+        def _():
+            wait_all(carry.at[p, pl.ds(0, span - 1)], c_recv.at[p])
+
+        @pl.when(core != p % cores)
+        def _():
+            wait_all(carry.at[p], c_recv.at[p])
 
     with jax.named_scope("decays0"):
         decays(0)
@@ -320,6 +351,7 @@
         send_states(0)
         for i in range(2):
             small_copy(i, core).start()
+        send_weight(0, 1)
 
         def here(g, c):
             pl.semaphore_signal(ready, inc=1, device_id=above(g), device_id_type=MESH)
@@ -328,18 +360,17 @@
         lax.fori_loop(0, group, here, 0)
         for k in range(chunks):
             pltpu.make_async_copy(columns(k), weight.at[core, k], weight_sem(k)).start()
-    for p in range(1, cores):
-        with jax.named_scope("in1"):
-            wait_all(held.at[pl.ds(0, 3), :, pl.ds(p * half, half)], in_sem.at[p + 2])
+    for p in range(1, parts):
+        if p % ways == 0:
+            with jax.named_scope("in1"):
+                side = p // ways
+                wait_all(held.at[pl.ds(0, 3), :, pl.ds(side * half, half)], in_sem.at[side + 2])
         with jax.named_scope("decays1"):
             decays(p)
         with jax.named_scope("send1"):
             send_states(p)
-    send_weight(0, 4)
-
-    @pl.when(group == 0)
-    def _():
-        send_weight(4, 5)
+            send_weight(p, p + 1 if p < parts - 1 else p + 2)
+    sent = parts + 1
 
     with jax.named_scope("in2"):
         wait_all(held.at[pl.ds(3, 2)], in_sem.at[cores + 2])
@@ -351,7 +382,7 @@
                 h * breadth // half, pl.ds(h % (half // breadth), 1), :
             ]
 
-    units = [(p, t) for p in range(cores) for t in range(quads)]
+    units = [(p, t) for p in range(parts) for t in range(quads)]
     done = 0
 
     def some_within(count):
@@ -362,7 +393,7 @@
         done += count
 
     some_within(4)
-    for p in range(cores):
+    for p in range(ways):
         with jax.named_scope("wait_states"):
             wait_all(inbox.at[p, some], s_recv.at[p])
         with jax.named_scope("scan"):
@@ -378,22 +409,20 @@
             @pl.when(group == 0)
             def _():
                 send_carry(p, nothing[0])
-                if p < cores - 1:
-                    send_weight(5 + 2 * p, 7 + 2 * p)
-                else:
-                    send_weight(3 + 2 * cores)
+                send_weight(sent + 2 * p, sent + 2 * p + 2 if p < ways - 1 else 2 * chunks)
 
             @pl.when(group > 0)
             def _():
-                send_weight(4 + 2 * p, 6 + 2 * p)
-
-        some_within(2 if p < cores - 1 else len(units))
+                send_weight(sent + 2 * p, sent + 2 * p + 2)
+
+        some_within(2 if p < ways - 1 else len(units))
     with jax.named_scope("take_group"):
         @pl.when(group > 0)
         def _():
-            for p in range(cores):
+            for p in range(ways):
+                at = sent + 2 * ways + p
                 send_carry(p, take_group(p))
-            send_weight(4 + 2 * cores)
+                send_weight(at, at + 1 if p < ways - 1 else 2 * chunks)
 
     def project(k, first, last):
         at = pl.ds(k * CHUNK, CHUNK)
@@ -406,40 +435,43 @@
         else:
             out_ref[:, at] = total.astype(BF16)
 
-    for p in range(cores - 1):
-        with jax.named_scope("wait_carry"):
-            wait_all(carry.at[p, some], c_recv.at[p])
-        with jax.named_scope("finish"):
-            finish(p)
+    early = parts - ways
+    with jax.named_scope("wait_carry"):
+        for p in range(early):
+            wait_carry(p)
+    with jax.named_scope("finish"):
+        finish(range(early))
     with jax.named_scope("wait_weight"):
         wait_all(weight.at[:, pl.ds(0, lead)], w_sem.at[0])
     with jax.named_scope("project_lead"):
         for k in range(lead - 2):
             project(k, 0, cores - 1)
     with jax.named_scope("wait_carry"):
-        wait_all(carry.at[cores - 1, some], c_recv.at[cores - 1])
+        for p in range(early, parts):
+            wait_carry(p)
     with jax.named_scope("finish"):
-        finish(cores - 1, range(lead - 2, lead))
+        finish(range(early, parts), range(lead - 2, lead))
     with jax.named_scope("project_led"):
         for k in range(lead):
             project(k, cores - 1, cores)
-    with jax.named_scope("wait_weight"):
-        for k in range(lead, chunks):
-            wait_all(weight.at[:, k], weight_sem(k))
-    with jax.named_scope("project_rest"):
-        for k in range(lead, chunks):
-            project(k, 0, cores)
+    for at in range(lead, chunks, 2):
+        pair = range(at, min(at + 2, chunks))
+        with jax.named_scope("wait_weight"):
+            for k in pair:
+                wait_all(weight.at[:, k], weight_sem(k))
+        with jax.named_scope("project_rest"):
+            for k in pair:
+                project(k, 0, cores)
 
     def drain_groups(g, c):
-        for p in range(cores):
+        for p in range(ways):
             group_copy(p, g, group).wait_send()
         return c
 
     with jax.named_scope("drain"):
         lax.fori_loop(group + 1, groups, drain_groups, 0)
-        for p in range(cores):
-            wait_all(outbox.at[p, some], s_send.at[p])
-            wait_all(cbox.at[p, some], c_send.at[p])
+        wait_all(inbox.at[:, some], s_send.at[0])
+        wait_all(cbox.at[:, some], c_send.at[0])
         wait_all(weight.at[other], w_send.at[0])
         for i in range(2):
             small_copy(i, core).wait_send()
@@ -449,8 +481,10 @@
     tokens, width = rec.shape
     breadth = reward.shape[1]
     half, depth = mapping.shape
-    blocks, chunks, members = tokens // BLOCK, depth // CHUNK, half // LANES
-    groups = n * cores // members
+    ways = WAYS
+    parts = ways * cores
+    blocks, chunks, span = tokens // BLOCK, depth // CHUNK, width // parts // LANES
+    members, groups = span * cores, n // span
     boxed = breadth + EXTRA
     dma = pltpu.SemaphoreType.DMA
     narrow = pltpu.VMEM((tokens, width), BF16)
@@ -467,23 +501,23 @@
             pltpu.VMEM((cores, chunks, half, CHUNK), BF16),
             pltpu.VMEM((1, width), F32),
             wide, narrow, narrow, narrow, wide, wide,
-            pltpu.VMEM((cores, max(blocks - 1, 1), members, breadth, LANES), BF16),
+            pltpu.VMEM((parts, max(blocks - 1, 1), span, breadth, LANES), BF16),
             pltpu.VMEM((blocks, 1, width), F32),
             pltpu.VMEM((blocks, 1, width), F32),
-            pltpu.VMEM((cores, members, boxed, LANES), BF16),
-            pltpu.VMEM((cores, members, boxed, LANES), BF16),
-            pltpu.VMEM((cores, members, breadth, LANES), F32),
-            pltpu.VMEM((cores, members, 1, LANES), F32),
-            pltpu.VMEM((cores, boxed, LANES), BF16),
-            pltpu.VMEM((cores, groups, boxed, LANES), BF16),
-            pltpu.VMEM((cores, members, breadth, LANES), BF16),
-            pltpu.VMEM((cores, members, breadth, LANES), BF16),
+            pltpu.VMEM((parts, span, boxed, LANES), BF16),
+            pltpu.VMEM((ways, members, boxed, LANES), BF16),
+            pltpu.VMEM((ways, members, breadth, LANES), F32),
+            pltpu.VMEM((ways, members, 1, LANES), F32),
+            pltpu.VMEM((ways, boxed, LANES), BF16),
+            pltpu.VMEM((ways, groups, boxed, LANES), BF16),
+            pltpu.VMEM((ways, members, breadth, LANES), BF16),
+            pltpu.VMEM((parts, span, breadth, LANES), BF16),
             narrow,
             pltpu.VMEM((tokens, depth), F32),
             dma((cores + 3,)), dma((2,)), dma((2,)), dma((2,)),
             dma((max(chunks - LEAD, 0) + 1,)), dma((1,)),
-            dma((cores,)), dma((cores,)), dma((cores, groups)), dma((cores, groups)),
-            dma((cores,)), dma((cores,)), pltpu.SemaphoreType.REGULAR,
+            dma((1,)), dma((ways,)), dma((ways, groups)), dma((ways, groups)),
+            dma((1,)), dma((parts,)), pltpu.SemaphoreType.REGULAR,
         ],
         compiler_params=pltpu.CompilerParams(
             collective_id=0, has_side_effects=True, vmem_limit_bytes=52 * 2**20

time: 23.2 us -> 22.5 us (0.970)
  Pallas kernels: 21.8 us -> 20.9 us
    pallas_call x1, Pallas kernels: 21.8 us -> 20.9 us  [shards(): pl.pallas_call(functools.partial(kernel, n, cores, breadth), out_shape=pl...]
where the time goes in v5:
time: 22.5 us; the launch traced here: 22.2 us
  Pallas kernels  20.9 us (93%)
  local copies, waits for them, and re-layouts  1.32 us (6%)
    pallas_call x1, Pallas kernels, shards(): pl.pallas_call(functools.partial(kernel, n, cores, breadth), out_shape=pl...  20.9 us
    unnamed x1, local copies, waits for them, and re-layouts  1.32 us

profile of v5, /device:TPU:17, one launch (start us, length us, event | category | flops | bytes accessed | tf_op | source)
XLA Modules:
  0.0 22.2 jit_solution(1339333662506172040)
XLA Ops:
  0.0 20.9 %shard_map.82 = bf16[256,4096]{1,0:T(8,128)(2,1)S(1)} custom-call(bf16[256,2048]{1,0:T(8,128)(2,1)} %rec_hbm.1, bf16[256,2048]{1,0:T(8,128)(2,1)} %key_hbm.1, bf16[256,2048]{1,0:T(8,128)(2,1)} %val_hbm.1, bf16[256,2048]{1,0:T(8,128)(2,1)} %fade_hbm.1, bf16[256,2048]{1,0:T(8,128)(2,1)} %gate_hbm.1, f32[16,64]{1,0:T(8,128)} %reward_hbm.1, f32[1,1024]{1,0:T(1,128)} %bitcast.1, ...), custom_call_target="tpu_custom_call" | custom-call | tf_op jit(solution)/shard_map/pallas_call | solution.py:492
  20.9 1.3 %copy.10 = bf16[256,4096]{1,0:T(8,128)(2,1)} copy(bf16[256,4096]{1,0:T(8,128)(2,1)S(1)} %shard_map.82) | data formatting | bytes 4194304

commit v6 on v5

--- a/solution.py
+++ b/solution.py
@@ -13,6 +13,7 @@
 CHUNK = 512
 LEAD = 4
 WAYS = 2
+TAIL = 2
 EXTRA = 8
 EPS = 1e-05
 MESH = pl.DeviceIdType.MESH
@@ -48,10 +49,10 @@
 def kernel(
     n, cores, breadth,
     rec_hbm, key_hbm, val_hbm, fade_hbm, gate_hbm, reward_hbm, gain_hbm, map_hbm,
-    out_ref,
-    held, rewards, gains, weight,
+    out_ref, gated, weight_tail,
+    held, rewards, gains, weight_head,
     reward_row, cumx, key_mid, centred, recs, local_out, swish, entering, pref_row, mid_row,
-    outbox, inbox, before, before_dec, gout, gin, cbox, carry, gated, partial,
+    outbox, inbox, before, before_dec, gout, gin, cbox, carry, partial,
     in_sem, p_local, p_send, p_recv, w_sem, w_send,
     s_send, s_recv, g_send, g_recv, c_send, c_recv, ready,
 ):
@@ -63,7 +64,8 @@
     ways = parts // cores
     lane = width // parts
     blocks, quads = tokens // BLOCK, lane // QUAD
-    chunks = weight.shape[1]
+    split = weight_head.shape[1]
+    chunks = split + weight_tail.shape[1]
     lead = min(LEAD, chunks)
     members = span * cores
     groups = n // span
@@ -120,6 +122,9 @@
     def columns(k):
         return map_hbm.at[:, pl.ds(k * CHUNK, CHUNK)]
 
+    def weight(side, k):
+        return weight_head.at[side, k] if k < split else weight_tail.at[side, k - split]
+
     def weight_sem(k):
         return w_sem.at[max(k - lead + 1, 0)]
 
@@ -127,7 +132,7 @@
         for piece in range(start, min(stop, 2 * chunks)):
             k, rows = piece // 2, pl.ds(piece % 2 * (half // 2), half // 2)
             pltpu.make_async_remote_copy(
-                src_ref=map_hbm.at[rows, pl.ds(k * CHUNK, CHUNK)], dst_ref=weight.at[core, k, rows],
+                src_ref=map_hbm.at[rows, pl.ds(k * CHUNK, CHUNK)], dst_ref=weight(core, k).at[rows],
                 send_sem=w_send.at[0], recv_sem=weight_sem(k),
                 device_id=(me, other), device_id_type=MESH,
             ).start()
@@ -305,7 +310,7 @@
     def group_copy(p, g, slot):
         return pltpu.make_async_remote_copy(
             src_ref=gout.at[p], dst_ref=gin.at[p, slot],
-            send_sem=g_send.at[p, g], recv_sem=g_recv.at[p, slot],
+            send_sem=g_send.at[0], recv_sem=g_recv.at[p, slot],
             device_id=above(g), device_id_type=MESH,
         )
 
@@ -359,7 +364,7 @@
 
         lax.fori_loop(0, group, here, 0)
         for k in range(chunks):
-            pltpu.make_async_copy(columns(k), weight.at[core, k], weight_sem(k)).start()
+            pltpu.make_async_copy(columns(k), weight(core, k), weight_sem(k)).start()
     for p in range(1, parts):
         if p % ways == 0:
             with jax.named_scope("in1"):
@@ -428,7 +433,7 @@
         at = pl.ds(k * CHUNK, CHUNK)
         total = partial[:, at] if first > 0 else None
         for p in range(first, last):
-            term = dot(gated[:, pl.ds(p * half, half)], weight[p, k])
+            term = dot(gated[:, pl.ds(p * half, half)], weight(p, k)[...])
             total = term if total is None else total + term
         if last < cores:
             partial[:, at] = total
@@ -442,7 +447,7 @@
     with jax.named_scope("finish"):
         finish(range(early))
     with jax.named_scope("wait_weight"):
-        wait_all(weight.at[:, pl.ds(0, lead)], w_sem.at[0])
+        wait_all(weight_head.at[:, pl.ds(0, lead)], w_sem.at[0])
     with jax.named_scope("project_lead"):
         for k in range(lead - 2):
             project(k, 0, cores - 1)
@@ -454,27 +459,44 @@
     with jax.named_scope("project_led"):
         for k in range(lead):
             project(k, cores - 1, cores)
-    for at in range(lead, chunks, 2):
-        pair = range(at, min(at + 2, chunks))
-        with jax.named_scope("wait_weight"):
-            for k in pair:
-                wait_all(weight.at[:, k], weight_sem(k))
-        with jax.named_scope("project_rest"):
-            for k in pair:
-                project(k, 0, cores)
-
-    def drain_groups(g, c):
-        for p in range(ways):
-            group_copy(p, g, group).wait_send()
-        return c
+    with jax.named_scope("wait_weight"):
+        for k in range(lead, split):
+            wait_all(weight_head.at[:, k], weight_sem(k))
+    with jax.named_scope("project_rest"):
+        for k in range(lead, split):
+            project(k, 0, cores)
+    with jax.named_scope("wait_weight"):
+        for k in range(split, chunks):
+            wait_all(weight_tail.at[:, k - split], weight_sem(k))
+
+    def drain_groups(g):
+        wait_all(gin.at[:, pl.ds(0, groups - 1 - g)], g_send.at[0])
 
     with jax.named_scope("drain"):
-        lax.fori_loop(group + 1, groups, drain_groups, 0)
+        for g in range(groups - 1):
+            pl.when(group == g)(functools.partial(drain_groups, g))
         wait_all(inbox.at[:, some], s_send.at[0])
         wait_all(cbox.at[:, some], c_send.at[0])
-        wait_all(weight.at[other], w_send.at[0])
+        wait_all(map_hbm, w_send.at[0])
         for i in range(2):
             small_copy(i, core).wait_send()
+
+
+def tail_kernel(done_ref, gated_ref, weight_ref, out_hbm, last, sem):
+    cores, tail, half, chunk = weight_ref.shape
+    done = done_ref.shape[1]
+    copies = [pltpu.make_async_copy(done_ref, out_hbm.at[:, pl.ds(0, done)], sem.at[0])]
+    copies[0].start()
+    for k in range(tail):
+        total = dot(gated_ref[:, pl.ds(0, half)], weight_ref[0, k])
+        for p in range(1, cores):
+            total = total + dot(gated_ref[:, pl.ds(p * half, half)], weight_ref[p, k])
+        last[k] = total.astype(BF16)
+        at = pl.ds(done + k * chunk, chunk)
+        copies.append(pltpu.make_async_copy(last.at[k], out_hbm.at[:, at], sem.at[k + 1]))
+        copies[-1].start()
+    for copy in copies:
+        copy.wait()
 
 
 def shards(n, cores, rec, key, val, fade, gate, reward, gain, mapping):
@@ -489,16 +511,23 @@
     dma = pltpu.SemaphoreType.DMA
     narrow = pltpu.VMEM((tokens, width), BF16)
     wide = pltpu.VMEM((tokens, width), F32)
-    return pl.pallas_call(
+    tail = min(TAIL, chunks - LEAD)
+    split = chunks - tail
+    vmem = pl.BlockSpec(memory_space=pltpu.VMEM)
+    done, gated, last = pl.pallas_call(
         functools.partial(kernel, n, cores, breadth),
-        out_shape=pltpu.VMEM((tokens, depth), BF16),
+        out_shape=(
+            pltpu.VMEM((tokens, split * CHUNK), BF16),
+            pltpu.VMEM((tokens, width), BF16),
+            pltpu.VMEM((cores, tail, half, CHUNK), BF16),
+        ),
         in_specs=[pl.BlockSpec(memory_space=pl.ANY)] * 8,
-        out_specs=pl.BlockSpec(memory_space=pltpu.VMEM),
+        out_specs=(vmem,) * 3,
         scratch_shapes=[
             pltpu.VMEM((5, tokens, width), BF16),
             pltpu.VMEM((cores,) + reward.shape, F32),
             pltpu.VMEM((cores, 1, half), F32),
-            pltpu.VMEM((cores, chunks, half, CHUNK), BF16),
+            pltpu.VMEM((cores, split, half, CHUNK), BF16),
             pltpu.VMEM((1, width), F32),
             wide, narrow, narrow, narrow, wide, wide,
             pltpu.VMEM((parts, max(blocks - 1, 1), span, breadth, LANES), BF16),
@@ -512,17 +541,24 @@
             pltpu.VMEM((ways, groups, boxed, LANES), BF16),
             pltpu.VMEM((ways, members, breadth, LANES), BF16),
             pltpu.VMEM((parts, span, breadth, LANES), BF16),
-            narrow,
-            pltpu.VMEM((tokens, depth), F32),
+            pltpu.VMEM((tokens, LEAD * CHUNK), F32),
             dma((cores + 3,)), dma((2,)), dma((2,)), dma((2,)),
             dma((max(chunks - LEAD, 0) + 1,)), dma((1,)),
-            dma((1,)), dma((ways,)), dma((ways, groups)), dma((ways, groups)),
+            dma((1,)), dma((ways,)), dma((1,)), dma((ways, groups)),
             dma((1,)), dma((parts,)), pltpu.SemaphoreType.REGULAR,
         ],
         compiler_params=pltpu.CompilerParams(
-            collective_id=0, has_side_effects=True, vmem_limit_bytes=52 * 2**20
+            collective_id=0, has_side_effects=True, vmem_limit_bytes=55 * 2**20
         ),
     )(rec, key, val, fade, gate, reward, gain.reshape(1, -1), mapping)
+    return pl.pallas_call(
+        tail_kernel,
+        out_shape=jax.ShapeDtypeStruct((tokens, depth), BF16),
+        in_specs=[vmem] * 3,
+        out_specs=pl.BlockSpec(memory_space=pl.ANY),
+        scratch_shapes=[pltpu.VMEM((tail, tokens, CHUNK), BF16), dma((tail + 1,))],
+        compiler_params=pltpu.CompilerParams(vmem_limit_bytes=16 * 2**20),
+    )(done, gated, last)
 
 
 def solution(mesh):

time: 22.5 us -> 21.8 us (0.969)
  local copies, waits for them, and re-layouts: 1.32 us -> 0 us
  Pallas kernels: 20.9 us -> 21.6 us
    unnamed x1 -> x0, local copies, waits for them, and re-layouts: 1.32 us -> none
    pallas_call x1 -> x2, Pallas kernels: 20.9 us -> 21.6 us  [the longest x1 19.6 us: shards(): pl.pallas_call(functools.partial(kernel, n, cores, breadth), out_shape=(p...]
where the time goes in v6:
time: 21.8 us; the launch traced here: 21.6 us
  Pallas kernels  21.6 us (99%)
    pallas_call x1, Pallas kernels, shards(): pl.pallas_call(functools.partial(kernel, n, cores, breadth), out_shape=(p...  19.6 us
    pallas_call x1, Pallas kernels, shards(): pl.pallas_call(tail_kernel, out_shape=jax.ShapeDtypeStruct((tokens, depth...  1.98 us

profile of v6, /device:TPU:17, one launch (start us, length us, event | category | flops | bytes accessed | tf_op | source)
XLA Modules:
  0.0 21.6 jit_solution(3270275517203121726)
XLA Ops:
  0.0 19.6 %shard_map.82 = (bf16[256,3072]{1,0:T(8,128)(2,1)S(1)}, bf16[256,2048]{1,0:T(8,128)(2,1)S(1)}, bf16[2,2,1024,512]{3,2,1,0:T(8,128)(2,1)S(1)}) custom-call(bf16[256,2048]{1,0:T(8,128)(2,1)} %rec_hbm.1, bf16[256,2048]{1,0:T(8,128)(2,1)} %key_hbm.1, bf16[256,2048]{1,0:T(8,128)(2,1)} %val_hbm.1, bf16[256,2048]{1,0:T(8,128)(2,1)} %fade_hbm.1, ...), custom_call_target="tpu_custom_call" | custom-call | tf_op jit(solution)/shard_map/pallas_call | solution.py:517
  19.6 2.0 %shard_map.83 = bf16[256,4096]{1,0:T(8,128)(2,1)} custom-call(bf16[256,3072]{1,0:T(8,128)(2,1)S(1)} %get-tuple-element.8.done_ref, bf16[256,2048]{1,0:T(8,128)(2,1)S(1)} %get-tuple-element.9.gated_ref, bf16[2,2,1024,512]{3,2,1,0:T(8,128)(2,1)S(1)} %get-tuple-element.10.weight_ref), custom_call_target="tpu_custom_call" | custom-call | tf_op jit(solution)/shard_map/pallas_call | solution.py:554

commit v7 on v6

--- a/solution.py
+++ b/solution.py
@@ -87,10 +87,11 @@
     for q in peers:
         pl.semaphore_signal(barrier, inc=1, device_id=place(q), device_id_type=MESH)
 
-    for p in range(cores):
+    pieces = [pl.ds(p * lane, lane) for p in range(ways)]
+    pieces += [pl.ds(side * half, half) for side in range(1, cores)]
+    for piece, at in enumerate(pieces):
         for i in (0, 2, 1):
-            at = pl.ds(p * half, half)
-            sem = in_sem.at[i if p == 0 else p + 2]
+            sem = in_sem.at[i if piece == 0 else piece + 2]
             pltpu.make_async_copy(sources[i].at[:, at], held.at[i, :, at], sem).start()
 
     def greet_above(g, c):
@@ -99,7 +100,7 @@
 
     lax.fori_loop(group + 1, groups, greet_above, 0)
     for i in range(3, 5):
-        pltpu.make_async_copy(sources[i], held.at[i], in_sem.at[cores + 2]).start()
+        pltpu.make_async_copy(sources[i], held.at[i], in_sem.at[len(pieces) + 2]).start()
 
     def wait_all(ref, sem):
         pltpu.make_async_copy(ref, ref, sem).wait()
@@ -165,7 +166,7 @@
 
     def arrive(p, i):
         if p == 0:
-            wait_all(held.at[i, :, pl.ds(0, half)], in_sem.at[i])
+            wait_all(held.at[i, :, pieces[0]], in_sem.at[i])
 
     def decays(p):
         cells = [(t, b) for t in range(quads) for b in range(blocks)]
@@ -246,27 +247,26 @@
                 local_out[at, pl.ds(p * lane + t * QUAD + j * LANES, LANES)] = o
 
     def finish(ps, between=()):
-        cells = [(p, t, b) for p in ps for t in range(quads) for b in range(blocks)]
-        states, outs, variances = {}, {}, {}
-        for p in ps:
-            for t in range(quads):
-                x, y = (split_heads(carry[p, 2 * t + j], low_s) for j in range(2))
-                none = jnp.zeros_like(x)
-                states[p, t] = jnp.concatenate(
-                    [jnp.concatenate([x, none], axis=1), jnp.concatenate([none, y], axis=1)], axis=0
-                )
-        for p, t, b in cells:
-            at, lanes = pl.ds(b * BLOCK, BLOCK), quad_lanes(p, t)
-            outs[p, t, b] = local_out[at, lanes] + dot_nt(recs[at, lanes], states[p, t])
-        for p, t, b in cells:
-            out = outs[p, t, b]
-            variances[p, t, b] = dot((out * out).astype(BF16), means)
+        cells = [(p, t) for p in ps for t in range(quads)]
+        states, outs = {}, {}
+        for p, t in cells:
+            x, y = (split_heads(carry[p, 2 * t + j], low_s) for j in range(2))
+            none = jnp.zeros_like(x)
+            states[p, t] = jnp.concatenate(
+                [jnp.concatenate([x, none], axis=1), jnp.concatenate([none, y], axis=1)], axis=0
+            )
+        for p, t in cells:
+            lanes = quad_lanes(p, t)
+            outs[p, t] = local_out[:, lanes] + dot_nt(recs[:, lanes], states[p, t])
+        squares = [(outs[cell] * outs[cell]).astype(BF16) for cell in cells]
+        variances = dot(jnp.concatenate(squares, axis=0), means)
         for k in between:
             project(k, 0, cores - 1)
-        for p, t, b in cells:
-            at, lanes = pl.ds(b * BLOCK, BLOCK), quad_lanes(p, t)
-            scale = lax.rsqrt(variances[p, t, b] + EPS) * swish[at, lanes]
-            gated[at, lanes] = (outs[p, t, b] * scale).astype(BF16)
+        for i, (p, t) in enumerate(cells):
+            lanes = quad_lanes(p, t)
+            variance = variances[i * tokens : (i + 1) * tokens]
+            scale = lax.rsqrt(variance + EPS) * swish[:, lanes]
+            gated[:, lanes] = (outs[p, t] * scale).astype(BF16)
 
     def send_states(p):
         way, owner = p // cores, p % cores
@@ -366,19 +366,23 @@
         for k in range(chunks):
             pltpu.make_async_copy(columns(k), weight(core, k), weight_sem(k)).start()
     for p in range(1, parts):
-        if p % ways == 0:
+        piece = p if p < ways else ways - 1 + p // ways
+        if p < ways or p % ways == 0:
             with jax.named_scope("in1"):
-                side = p // ways
-                wait_all(held.at[pl.ds(0, 3), :, pl.ds(side * half, half)], in_sem.at[side + 2])
+                wait_all(held.at[pl.ds(0, 3), :, pieces[piece]], in_sem.at[piece + 2])
         with jax.named_scope("decays1"):
             decays(p)
         with jax.named_scope("send1"):
             send_states(p)
-            send_weight(p, p + 1 if p < parts - 1 else p + 2)
-    sent = parts + 1
+            send_weight(p, p + 1)
+    sent = parts
+
+    @pl.when(group > 0)
+    def _():
+        send_weight(sent, sent + 1)
 
     with jax.named_scope("in2"):
-        wait_all(held.at[pl.ds(3, 2)], in_sem.at[cores + 2])
+        wait_all(held.at[pl.ds(3, 2)], in_sem.at[len(pieces) + 2])
         for i in range(2):
             small_local[i].wait()
             small_copy(i, other).wait_recv()
@@ -414,18 +418,18 @@
             @pl.when(group == 0)
             def _():
                 send_carry(p, nothing[0])
-                send_weight(sent + 2 * p, sent + 2 * p + 2 if p < ways - 1 else 2 * chunks)
+                send_weight(sent + p, sent + p + 1 if p < ways - 1 else 2 * chunks)
 
             @pl.when(group > 0)
             def _():
-                send_weight(sent + 2 * p, sent + 2 * p + 2)
+                send_weight(sent + 2 * p + 1, sent + 2 * p + 3)
 
         some_within(2 if p < ways - 1 else len(units))
     with jax.named_scope("take_group"):
         @pl.when(group > 0)
         def _():
             for p in range(ways):
-                at = sent + 2 * ways + p
+                at = sent + 2 * ways + p + 1
                 send_carry(p, take_group(p))
                 send_weight(at, at + 1 if p < ways - 1 else 2 * chunks)
 
@@ -542,7 +546,7 @@
             pltpu.VMEM((ways, members, breadth, LANES), BF16),
             pltpu.VMEM((parts, span, breadth, LANES), BF16),
             pltpu.VMEM((tokens, LEAD * CHUNK), F32),
-            dma((cores + 3,)), dma((2,)), dma((2,)), dma((2,)),
+            dma((ways + cores + 2,)), dma((2,)), dma((2,)), dma((2,)),
             dma((max(chunks - LEAD, 0) + 1,)), dma((1,)),
             dma((1,)), dma((ways,)), dma((1,)), dma((ways, groups)),
             dma((1,)), dma((parts,)), pltpu.SemaphoreType.REGULAR,

time: 21.8 us -> 21.5 us (0.986)
  Pallas kernels: 21.6 us -> 21.3 us
    pallas_call x1, Pallas kernels: 19.6 us -> 19.3 us  [shards(): pl.pallas_call(functools.partial(kernel, n, cores, breadth), out_shape=(p...]
where the time goes in v7:
time: 21.5 us; the launch traced here: 21.3 us
  Pallas kernels  21.3 us (99%)
    pallas_call x1, Pallas kernels, shards(): pl.pallas_call(functools.partial(kernel, n, cores, breadth), out_shape=(p...  19.3 us
    pallas_call x1, Pallas kernels, shards(): pl.pallas_call(tail_kernel, out_shape=jax.ShapeDtypeStruct((tokens, depth...  1.98 us

profile of v7, /device:TPU:17, one launch (start us, length us, event | category | flops | bytes accessed | tf_op | source)
XLA Modules:
  0.0 21.3 jit_solution(10919861324639153873)
XLA Ops:
  0.0 19.3 %shard_map.82 = (bf16[256,3072]{1,0:T(8,128)(2,1)S(1)}, bf16[256,2048]{1,0:T(8,128)(2,1)S(1)}, bf16[2,2,1024,512]{3,2,1,0:T(8,128)(2,1)S(1)}) custom-call(bf16[256,2048]{1,0:T(8,128)(2,1)} %rec_hbm.1, bf16[256,2048]{1,0:T(8,128)(2,1)} %key_hbm.1, bf16[256,2048]{1,0:T(8,128)(2,1)} %val_hbm.1, bf16[256,2048]{1,0:T(8,128)(2,1)} %fade_hbm.1, ...), custom_call_target="tpu_custom_call" | custom-call | tf_op jit(solution)/shard_map/pallas_call | solution.py:521
  19.3 2.0 %shard_map.83 = bf16[256,4096]{1,0:T(8,128)(2,1)} custom-call(bf16[256,3072]{1,0:T(8,128)(2,1)S(1)} %get-tuple-element.8.done_ref, bf16[256,2048]{1,0:T(8,128)(2,1)S(1)} %get-tuple-element.9.gated_ref, bf16[2,2,1024,512]{3,2,1,0:T(8,128)(2,1)S(1)} %get-tuple-element.10.weight_ref), custom_call_target="tpu_custom_call" | custom-call | tf_op jit(solution)/shard_map/pallas_call | solution.py:558

commit v8 on v7

--- a/solution.py
+++ b/solution.py
@@ -127,7 +127,7 @@
         return weight_head.at[side, k] if k < split else weight_tail.at[side, k - split]
 
     def weight_sem(k):
-        return w_sem.at[max(k - lead + 1, 0)]
+        return w_sem.at[0 if k < lead else 1 if k < split else 2]
 
     def send_weight(start, stop=2 * chunks):
         for piece in range(start, min(stop, 2 * chunks)):
@@ -335,19 +335,10 @@
         for q in peers:
             pltpu.make_async_remote_copy(
                 src_ref=cbox.at[way, q], dst_ref=carry.at[p, chip],
-                send_sem=c_send.at[0], recv_sem=c_recv.at[p],
+                send_sem=c_send.at[0], recv_sem=c_recv.at[p // ways],
                 device_id=place(q), device_id_type=MESH,
             ).start()
         carry[p, chip] = cbox[way, r]
-
-    def wait_carry(p):
-        @pl.when(core == p % cores)
-        def _():
-            wait_all(carry.at[p, pl.ds(0, span - 1)], c_recv.at[p])
-
-        @pl.when(core != p % cores)
-        def _():
-            wait_all(carry.at[p], c_recv.at[p])
 
     with jax.named_scope("decays0"):
         decays(0)
@@ -374,12 +365,8 @@
             decays(p)
         with jax.named_scope("send1"):
             send_states(p)
-            send_weight(p, p + 1)
-    sent = parts
-
-    @pl.when(group > 0)
-    def _():
-        send_weight(sent, sent + 1)
+            send_weight(p, p + 1 if p < parts - 1 else p + 2)
+    sent = parts + 1
 
     with jax.named_scope("in2"):
         wait_all(held.at[pl.ds(3, 2)], in_sem.at[len(pieces) + 2])
@@ -418,18 +405,18 @@
             @pl.when(group == 0)
             def _():
                 send_carry(p, nothing[0])
-                send_weight(sent + p, sent + p + 1 if p < ways - 1 else 2 * chunks)
+                send_weight(sent + 2 * p, sent + 2 * p + 2 if p < ways - 1 else 2 * chunks)
 
             @pl.when(group > 0)
             def _():
-                send_weight(sent + 2 * p + 1, sent + 2 * p + 3)
+                send_weight(sent + 2 * p, sent + 2 * p + 2)
 
         some_within(2 if p < ways - 1 else len(units))
     with jax.named_scope("take_group"):
         @pl.when(group > 0)
         def _():
             for p in range(ways):
-                at = sent + 2 * ways + p + 1
+                at = sent + 2 * ways + p
                 send_carry(p, take_group(p))
                 send_weight(at, at + 1 if p < ways - 1 else 2 * chunks)
 
@@ -445,33 +432,27 @@
             out_ref[:, at] = total.astype(BF16)
 
     early = parts - ways
+    with jax.named_scope("wait_weight"):
+        wait_all(weight_head.at[:, pl.ds(0, lead)], w_sem.at[0])
     with jax.named_scope("wait_carry"):
-        for p in range(early):
-            wait_carry(p)
+        for side in range(cores - 1):
+            wait_all(cbox.at[0, some], c_recv.at[side])
     with jax.named_scope("finish"):
         finish(range(early))
-    with jax.named_scope("wait_weight"):
-        wait_all(weight_head.at[:, pl.ds(0, lead)], w_sem.at[0])
-    with jax.named_scope("project_lead"):
         for k in range(lead - 2):
             project(k, 0, cores - 1)
+    with jax.named_scope("wait_weight"):
+        wait_all(weight_head.at[:, pl.ds(lead, split - lead)], w_sem.at[1])
     with jax.named_scope("wait_carry"):
-        for p in range(early, parts):
-            wait_carry(p)
-    with jax.named_scope("finish"):
+        wait_all(cbox.at[0, some], c_recv.at[cores - 1])
+    with jax.named_scope("project"):
         finish(range(early, parts), range(lead - 2, lead))
-    with jax.named_scope("project_led"):
         for k in range(lead):
             project(k, cores - 1, cores)
-    with jax.named_scope("wait_weight"):
-        for k in range(lead, split):
-            wait_all(weight_head.at[:, k], weight_sem(k))
-    with jax.named_scope("project_rest"):
         for k in range(lead, split):
             project(k, 0, cores)
     with jax.named_scope("wait_weight"):
-        for k in range(split, chunks):
-            wait_all(weight_tail.at[:, k - split], weight_sem(k))
+        wait_all(weight_tail, w_sem.at[2])
 
     def drain_groups(g):
         wait_all(gin.at[:, pl.ds(0, groups - 1 - g)], g_send.at[0])
@@ -547,9 +528,9 @@
             pltpu.VMEM((parts, span, breadth, LANES), BF16),
             pltpu.VMEM((tokens, LEAD * CHUNK), F32),
             dma((ways + cores + 2,)), dma((2,)), dma((2,)), dma((2,)),
-            dma((max(chunks - LEAD, 0) + 1,)), dma((1,)),
+            dma((3,)), dma((1,)),
             dma((1,)), dma((ways,)), dma((1,)), dma((ways, groups)),
-            dma((1,)), dma((parts,)), pltpu.SemaphoreType.REGULAR,
+            dma((1,)), dma((cores,)), pltpu.SemaphoreType.REGULAR,
         ],
         compiler_params=pltpu.CompilerParams(
             collective_id=0, has_side_effects=True, vmem_limit_bytes=55 * 2**20

time: 21.5 us -> 21.1 us (0.981)
  Pallas kernels: 21.3 us -> 20.9 us
    pallas_call x1, Pallas kernels: 19.3 us -> 19 us  [shards(): pl.pallas_call(functools.partial(kernel, n, cores, breadth), out_shape=(p...]
where the time goes in v8:
time: 21.1 us; the launch traced here: 20.9 us
  Pallas kernels  20.9 us (99%)
    pallas_call x1, Pallas kernels, shards(): pl.pallas_call(functools.partial(kernel, n, cores, breadth), out_shape=(p...  19 us
    pallas_call x1, Pallas kernels, shards(): pl.pallas_call(tail_kernel, out_shape=jax.ShapeDtypeStruct((tokens, depth...  1.98 us

profile of v8, /device:TPU:17, one launch (start us, length us, event | category | flops | bytes accessed | tf_op | source)
XLA Modules:
  0.0 20.9 jit_solution(5049467973744430288)
XLA Ops:
  0.0 19.0 %shard_map.82 = (bf16[256,3072]{1,0:T(8,128)(2,1)S(1)}, bf16[256,2048]{1,0:T(8,128)(2,1)S(1)}, bf16[2,2,1024,512]{3,2,1,0:T(8,128)(2,1)S(1)}) custom-call(bf16[256,2048]{1,0:T(8,128)(2,1)} %rec_hbm.1, bf16[256,2048]{1,0:T(8,128)(2,1)} %key_hbm.1, bf16[256,2048]{1,0:T(8,128)(2,1)} %val_hbm.1, bf16[256,2048]{1,0:T(8,128)(2,1)} %fade_hbm.1, ...), custom_call_target="tpu_custom_call" | custom-call | tf_op jit(solution)/shard_map/pallas_call | solution.py:502
  19.0 2.0 %shard_map.83 = bf16[256,4096]{1,0:T(8,128)(2,1)} custom-call(bf16[256,3072]{1,0:T(8,128)(2,1)S(1)} %get-tuple-element.8.done_ref, bf16[256,2048]{1,0:T(8,128)(2,1)S(1)} %get-tuple-element.9.gated_ref, bf16[2,2,1024,512]{3,2,1,0:T(8,128)(2,1)S(1)} %get-tuple-element.10.weight_ref), custom_call_target="tpu_custom_call" | custom-call | tf_op jit(solution)/shard_map/pallas_call | solution.py:539

commit v9 on v8

--- a/solution.py
+++ b/solution.py
@@ -61,6 +61,7 @@
     tokens, width = held.shape[1:]
     half = width // cores
     parts, span = outbox.shape[:2]
+    owner = cores - 1
     ways = parts // cores
     lane = width // parts
     blocks, quads = tokens // BLOCK, lane // QUAD
@@ -87,8 +88,7 @@
     for q in peers:
         pl.semaphore_signal(barrier, inc=1, device_id=place(q), device_id_type=MESH)
 
-    pieces = [pl.ds(p * lane, lane) for p in range(ways)]
-    pieces += [pl.ds(side * half, half) for side in range(1, cores)]
+    pieces = [pl.ds(side * half, half) for side in range(cores)]
     for piece, at in enumerate(pieces):
         for i in (0, 2, 1):
             sem = in_sem.at[i if piece == 0 else piece + 2]
@@ -164,14 +164,16 @@
     def quad_lanes(p, t):
         return pl.ds(p * lane + t * QUAD, QUAD)
 
-    def arrive(p, i):
-        if p == 0:
+    def arrive(side, i):
+        if side == 0:
             wait_all(held.at[i, :, pieces[0]], in_sem.at[i])
 
-    def decays(p):
-        cells = [(t, b) for t in range(quads) for b in range(blocks)]
+    def decays(side):
+        turns = range(ways * quads)
+        cells = [(t, b) for t in turns for b in range(blocks)]
+        p = side * ways
         cums, vbs, kms, products = {}, {}, {}, {}
-        arrive(p, 0)
+        arrive(side, 0)
         for t, b in cells:
             at, lanes = pl.ds(b * BLOCK, BLOCK), quad_lanes(p, t)
             log_decay = -jnp.exp(fade[at, lanes].astype(F32))
@@ -180,12 +182,12 @@
             cum = dot(incl, jnp.concatenate([hi, lo], axis=0))
             cumx[at, lanes] = cum - log_decay
             cums[t, b] = cum
-        arrive(p, 2)
+        arrive(side, 2)
         for t, b in cells:
             at, lanes = pl.ds(b * BLOCK, BLOCK), quad_lanes(p, t)
             vbs[t, b] = dot(val[at, lanes], centre).astype(BF16)
             centred[at, lanes] = vbs[t, b]
-        arrive(p, 1)
+        arrive(side, 1)
         for t, b in cells:
             at, lanes = pl.ds(b * BLOCK, BLOCK), quad_lanes(p, t)
             mid = cums[t, b][BLOCK // 2 - 1 : BLOCK // 2]
@@ -195,7 +197,7 @@
         for t, b in cells:
             for j, cut in enumerate(cuts):
                 products[t, b, j] = dot_tn(vbs[t, b][:, cut], kms[t, b][:, cut])
-        for t in range(quads):
+        for t in turns:
             lanes = quad_lanes(p, t)
             states = [jnp.zeros((breadth, LANES), F32) for _ in range(2)]
             pref = jnp.zeros((1, QUAD), F32)
@@ -206,15 +208,15 @@
                 pref_row[b, :, lanes] = pref
                 for j, cut in enumerate(cuts):
                     if b > 0:
-                        entering[p, b - 1, 2 * t + j] = (states[j] * begin[:, cut]).astype(BF16)
+                        entering[p + t // quads, b - 1, t % quads * 2 + j] = (states[j] * begin[:, cut]).astype(BF16)
                     product = products[t, b, j]
                     own = jnp.where(low_s, product[:breadth], product[breadth:])
                     states[j] = states[j] * whole[:, cut] + own * end[:, cut]
                 pref = pref + total
             gone = jnp.exp(pref)
             for j, cut in enumerate(cuts):
-                outbox[p, 2 * t + j, state_rows, :] = states[j].astype(BF16)
-                outbox[p, 2 * t + j, decay_rows, :] = pack_rows(gone[:, cut])
+                outbox[p + t // quads, t % quads * 2 + j, state_rows, :] = states[j].astype(BF16)
+                outbox[p + t // quads, t % quads * 2 + j, decay_rows, :] = pack_rows(gone[:, cut])
 
     def within(units):
         cells = [(p, t, b) for p, t in units for b in range(blocks)]
@@ -269,25 +271,23 @@
             gated[:, lanes] = (outs[p, t] * scale).astype(BF16)
 
     def send_states(p):
-        way, owner = p // cores, p % cores
-        for t in chips[:-1]:
+        def send(t):
             pltpu.make_async_remote_copy(
-                src_ref=outbox.at[p, t], dst_ref=inbox.at[way, r],
-                send_sem=s_send.at[0], recv_sem=s_recv.at[way],
+                src_ref=outbox.at[p, t], dst_ref=inbox.at[p, r],
+                send_sem=s_send.at[0], recv_sem=s_recv.at[p],
                 device_id=(group * span + t, owner), device_id_type=MESH,
             ).start()
 
+        for t in chips[:-1]:
+            send(t)
+
         @pl.when(core == owner)
         def _():
-            inbox[way, r] = outbox[p, chip]
+            inbox[p, r] = outbox[p, chip]
 
         @pl.when(core != owner)
         def _():
-            pltpu.make_async_remote_copy(
-                src_ref=outbox.at[p, chip], dst_ref=inbox.at[way, r],
-                send_sem=s_send.at[0], recv_sem=s_recv.at[way],
-                device_id=(me, owner), device_id_type=MESH,
-            ).start()
+            send(chip)
 
     some = pl.ds(0, members - 1)
 
@@ -329,7 +329,7 @@
         return lax.fori_loop(0, group, body, nothing)[0]
 
     def send_carry(way, came):
-        p = way * cores + core
+        p = way
         for j in range(members):
             cbox[way, j] = (came * before_dec[way, j] + before[way, j]).astype(BF16)
         for q in peers:
@@ -344,7 +344,8 @@
         decays(0)
     with jax.named_scope("barrier"):
         pl.semaphore_wait(barrier, members - 1 + group)
-        send_states(0)
+        for p in range(ways):
+            send_states(p)
         for i in range(2):
             small_copy(i, core).start()
         send_weight(0, 1)
@@ -353,20 +354,26 @@
             pl.semaphore_signal(ready, inc=1, device_id=above(g), device_id_type=MESH)
             return c
 
-        lax.fori_loop(0, group, here, 0)
+        @pl.when(core == owner)
+        def _():
+            lax.fori_loop(0, group, here, 0)
+
         for k in range(chunks):
             pltpu.make_async_copy(columns(k), weight(core, k), weight_sem(k)).start()
-    for p in range(1, parts):
-        piece = p if p < ways else ways - 1 + p // ways
-        if p < ways or p % ways == 0:
-            with jax.named_scope("in1"):
-                wait_all(held.at[pl.ds(0, 3), :, pieces[piece]], in_sem.at[piece + 2])
+    for side in range(1, cores):
+        with jax.named_scope("in1"):
+            wait_all(held.at[pl.ds(0, 3), :, pieces[side]], in_sem.at[side + 2])
         with jax.named_scope("decays1"):
-            decays(p)
+            decays(side)
         with jax.named_scope("send1"):
-            send_states(p)
-            send_weight(p, p + 1 if p < parts - 1 else p + 2)
-    sent = parts + 1
+            for p in range(side * ways, side * ways + ways):
+                send_states(p)
+    sent = 5
+    send_weight(1, sent)
+
+    @pl.when(core != owner)
+    def _():
+        send_weight(sent)
 
     with jax.named_scope("in2"):
         wait_all(held.at[pl.ds(3, 2)], in_sem.at[len(pieces) + 2])
@@ -389,12 +396,13 @@
         done += count
 
     some_within(4)
-    for p in range(ways):
-        with jax.named_scope("wait_states"):
-            wait_all(inbox.at[p, some], s_recv.at[p])
-        with jax.named_scope("scan"):
-            scan(p)
-        with jax.named_scope("send_group"):
+    for p in range(parts):
+        @pl.when(core == owner)
+        def _():
+            with jax.named_scope("wait_states"):
+                wait_all(inbox.at[p, some], s_recv.at[p])
+            with jax.named_scope("scan"):
+                scan(p)
             if p == 0:
                 @pl.when(group < groups - 1)
                 def _():
@@ -405,20 +413,24 @@
             @pl.when(group == 0)
             def _():
                 send_carry(p, nothing[0])
-                send_weight(sent + 2 * p, sent + 2 * p + 2 if p < ways - 1 else 2 * chunks)
-
-            @pl.when(group > 0)
-            def _():
-                send_weight(sent + 2 * p, sent + 2 * p + 2)
-
-        some_within(2 if p < ways - 1 else len(units))
-    with jax.named_scope("take_group"):
+
+            send_weight(sent + p, sent + p + 1)
+
+        if p % 2:
+            some_within(2)
+    sent += parts
+
+    @pl.when(core == owner)
+    def _():
         @pl.when(group > 0)
         def _():
-            for p in range(ways):
-                at = sent + 2 * ways + p
-                send_carry(p, take_group(p))
-                send_weight(at, at + 1 if p < ways - 1 else 2 * chunks)
+            for p in range(parts):
+                with jax.named_scope("take_group"):
+                    came = take_group(p)
+                with jax.named_scope("send_carry"):
+                    send_carry(p, came)
+
+        send_weight(sent)
 
     def project(k, first, last):
         at = pl.ds(k * CHUNK, CHUNK)
@@ -432,11 +444,21 @@
             out_ref[:, at] = total.astype(BF16)
 
     early = parts - ways
+
+    def wait_carry(side):
+        @pl.when(core == owner)
+        def _():
+            wait_all(carry.at[pl.ds(0, ways), pl.ds(0, span - 1)], c_recv.at[side])
+
+        @pl.when(core != owner)
+        def _():
+            wait_all(carry.at[pl.ds(0, ways)], c_recv.at[side])
+
     with jax.named_scope("wait_weight"):
         wait_all(weight_head.at[:, pl.ds(0, lead)], w_sem.at[0])
     with jax.named_scope("wait_carry"):
         for side in range(cores - 1):
-            wait_all(cbox.at[0, some], c_recv.at[side])
+            wait_carry(side)
     with jax.named_scope("finish"):
         finish(range(early))
         for k in range(lead - 2):
@@ -444,7 +466,7 @@
     with jax.named_scope("wait_weight"):
         wait_all(weight_head.at[:, pl.ds(lead, split - lead)], w_sem.at[1])
     with jax.named_scope("wait_carry"):
-        wait_all(cbox.at[0, some], c_recv.at[cores - 1])
+        wait_carry(cores - 1)
     with jax.named_scope("project"):
         finish(range(early, parts), range(lead - 2, lead))
         for k in range(lead):
@@ -458,10 +480,17 @@
         wait_all(gin.at[:, pl.ds(0, groups - 1 - g)], g_send.at[0])
 
     with jax.named_scope("drain"):
-        for g in range(groups - 1):
-            pl.when(group == g)(functools.partial(drain_groups, g))
-        wait_all(inbox.at[:, some], s_send.at[0])
-        wait_all(cbox.at[:, some], c_send.at[0])
+        @pl.when(core == owner)
+        def _():
+            for g in range(groups - 1):
+                pl.when(group == g)(functools.partial(drain_groups, g))
+            wait_all(outbox.at[:, pl.ds(0, span - 1)], s_send.at[0])
+            wait_all(cbox.at[:, some], c_send.at[0])
+
+        @pl.when(core != owner)
+        def _():
+            wait_all(outbox, s_send.at[0])
+
         wait_all(map_hbm, w_send.at[0])
         for i in range(2):
             small_copy(i, core).wait_send()
@@ -519,17 +548,17 @@
             pltpu.VMEM((blocks, 1, width), F32),
             pltpu.VMEM((blocks, 1, width), F32),
             pltpu.VMEM((parts, span, boxed, LANES), BF16),
-            pltpu.VMEM((ways, members, boxed, LANES), BF16),
-            pltpu.VMEM((ways, members, breadth, LANES), F32),
-            pltpu.VMEM((ways, members, 1, LANES), F32),
-            pltpu.VMEM((ways, boxed, LANES), BF16),
-            pltpu.VMEM((ways, groups, boxed, LANES), BF16),
-            pltpu.VMEM((ways, members, breadth, LANES), BF16),
+            pltpu.VMEM((parts, members, boxed, LANES), BF16),
+            pltpu.VMEM((parts, members, breadth, LANES), F32),
+            pltpu.VMEM((parts, members, 1, LANES), F32),
+            pltpu.VMEM((parts, boxed, LANES), BF16),
+            pltpu.VMEM((parts, groups, boxed, LANES), BF16),
+            pltpu.VMEM((parts, members, breadth, LANES), BF16),
             pltpu.VMEM((parts, span, breadth, LANES), BF16),
             pltpu.VMEM((tokens, LEAD * CHUNK), F32),
-            dma((ways + cores + 2,)), dma((2,)), dma((2,)), dma((2,)),
+            dma((cores + 3,)), dma((2,)), dma((2,)), dma((2,)),
             dma((3,)), dma((1,)),
-            dma((1,)), dma((ways,)), dma((1,)), dma((ways, groups)),
+            dma((1,)), dma((parts,)), dma((1,)), dma((parts, groups)),
             dma((1,)), dma((cores,)), pltpu.SemaphoreType.REGULAR,
         ],
         compiler_params=pltpu.CompilerParams(

time: 21.1 us -> 20.1 us (0.953)
  Pallas kernels: 20.9 us -> 19.8 us
    pallas_call x1, Pallas kernels: 19 us -> 17.9 us  [shards(): pl.pallas_call(functools.partial(kernel, n, cores, breadth), out_shape=(p...]
where the time goes in v9:
time: 20.1 us; the launch traced here: 19.9 us
  Pallas kernels  19.8 us (99%)
    pallas_call x1, Pallas kernels, shards(): pl.pallas_call(functools.partial(kernel, n, cores, breadth), out_shape=(p...  17.9 us
    pallas_call x1, Pallas kernels, shards(): pl.pallas_call(tail_kernel, out_shape=jax.ShapeDtypeStruct((tokens, depth...  1.98 us

profile of v9, /device:TPU:17, one launch (start us, length us, event | category | flops | bytes accessed | tf_op | source)
XLA Modules:
  0.0 19.9 jit_solution(9739949934682498929)
XLA Ops:
  0.0 17.9 %shard_map.82 = (bf16[256,3072]{1,0:T(8,128)(2,1)S(1)}, bf16[256,2048]{1,0:T(8,128)(2,1)S(1)}, bf16[2,2,1024,512]{3,2,1,0:T(8,128)(2,1)S(1)}) custom-call(bf16[256,2048]{1,0:T(8,128)(2,1)} %rec_hbm.1, bf16[256,2048]{1,0:T(8,128)(2,1)} %key_hbm.1, bf16[256,2048]{1,0:T(8,128)(2,1)} %val_hbm.1, bf16[256,2048]{1,0:T(8,128)(2,1)} %fade_hbm.1, ...), custom_call_target="tpu_custom_call" | custom-call | tf_op jit(solution)/shard_map/pallas_call | solution.py:531
  17.9 2.0 %shard_map.83 = bf16[256,4096]{1,0:T(8,128)(2,1)} custom-call(bf16[256,3072]{1,0:T(8,128)(2,1)S(1)} %get-tuple-element.8.done_ref, bf16[256,2048]{1,0:T(8,128)(2,1)S(1)} %get-tuple-element.9.gated_ref, bf16[2,2,1024,512]{3,2,1,0:T(8,128)(2,1)S(1)} %get-tuple-element.10.weight_ref), custom_call_target="tpu_custom_call" | custom-call | tf_op jit(solution)/shard_map/pallas_call | solution.py:568

commit v10 on v9

--- a/solution.py
+++ b/solution.py
@@ -13,7 +13,7 @@
 CHUNK = 512
 LEAD = 4
 WAYS = 2
-TAIL = 2
+TAIL = 1
 EXTRA = 8
 EPS = 1e-05
 MESH = pl.DeviceIdType.MESH
@@ -413,12 +413,15 @@
             @pl.when(group == 0)
             def _():
                 send_carry(p, nothing[0])
-
-            send_weight(sent + p, sent + p + 1)
+                send_weight(sent + p, sent + p + 1 if p < parts - 1 else 2 * chunks)
+
+            @pl.when(group > 0)
+            def _():
+                send_weight(sent + p, sent + p + 1 if p < parts - 1 else sent + p + 2)
 
         if p % 2:
             some_within(2)
-    sent += parts
+    sent += parts + 1
 
     @pl.when(core == owner)
     def _():
@@ -429,8 +432,7 @@
                     came = take_group(p)
                 with jax.named_scope("send_carry"):
                     send_carry(p, came)
-
-        send_weight(sent)
+            send_weight(sent)
 
     def project(k, first, last):
         at = pl.ds(k * CHUNK, CHUNK)
@@ -461,16 +463,17 @@
             wait_carry(side)
     with jax.named_scope("finish"):
         finish(range(early))
-        for k in range(lead - 2):
+        for k in range(lead - 1):
             project(k, 0, cores - 1)
-    with jax.named_scope("wait_weight"):
-        wait_all(weight_head.at[:, pl.ds(lead, split - lead)], w_sem.at[1])
     with jax.named_scope("wait_carry"):
         wait_carry(cores - 1)
     with jax.named_scope("project"):
-        finish(range(early, parts), range(lead - 2, lead))
+        finish(range(early, parts), range(lead - 1, lead))
         for k in range(lead):
             project(k, cores - 1, cores)
+    with jax.named_scope("wait_weight"):
+        wait_all(weight_head.at[:, pl.ds(lead, split - lead)], w_sem.at[1])
+    with jax.named_scope("project_rest"):
         for k in range(lead, split):
             project(k, 0, cores)
     with jax.named_scope("wait_weight"):

time: 20.1 us -> 19.9 us (0.990)
    pallas_call x1, Pallas kernels: 1.98 us -> 1.43 us  [shards(): pl.pallas_call(tail_kernel, out_shape=jax.ShapeDtypeStruct((tokens, depth...]
    pallas_call x1, Pallas kernels: 17.9 us -> 18.3 us  [shards(): pl.pallas_call(functools.partial(kernel, n, cores, breadth), out_shape=(p...]
where the time goes in v10:
time: 19.9 us; the launch traced here: 19.7 us
  Pallas kernels  19.7 us (99%)
    pallas_call x1, Pallas kernels, shards(): pl.pallas_call(functools.partial(kernel, n, cores, breadth), out_shape=(p...  18.3 us
    pallas_call x1, Pallas kernels, shards(): pl.pallas_call(tail_kernel, out_shape=jax.ShapeDtypeStruct((tokens, depth...  1.43 us

profile of v10, /device:TPU:17, one launch (start us, length us, event | category | flops | bytes accessed | tf_op | source)
XLA Modules:
  0.0 19.7 jit_solution(10808963389206955758)
XLA Ops:
  0.0 18.3 %shard_map.82 = (bf16[256,3584]{1,0:T(8,128)(2,1)S(1)}, bf16[256,2048]{1,0:T(8,128)(2,1)S(1)}, bf16[2,1,1024,512]{3,2,1,0:T(8,128)(2,1)S(1)}) custom-call(bf16[256,2048]{1,0:T(8,128)(2,1)} %rec_hbm.1, bf16[256,2048]{1,0:T(8,128)(2,1)} %key_hbm.1, bf16[256,2048]{1,0:T(8,128)(2,1)} %val_hbm.1, bf16[256,2048]{1,0:T(8,128)(2,1)} %fade_hbm.1, ...), custom_call_target="tpu_custom_call" | custom-call | tf_op jit(solution)/shard_map/pallas_call | solution.py:534
  18.3 1.4 %shard_map.83 = bf16[256,4096]{1,0:T(8,128)(2,1)} custom-call(bf16[256,3584]{1,0:T(8,128)(2,1)S(1)} %get-tuple-element.8.done_ref, bf16[256,2048]{1,0:T(8,128)(2,1)S(1)} %get-tuple-element.9.gated_ref, bf16[2,1,1024,512]{3,2,1,0:T(8,128)(2,1)S(1)} %get-tuple-element.10.weight_ref), custom_call_target="tpu_custom_call" | custom-call | tf_op jit(solution)/shard_map/pallas_call | solution.py:571

commit v11 on v10

--- a/solution.py
+++ b/solution.py
@@ -335,7 +335,7 @@
         for q in peers:
             pltpu.make_async_remote_copy(
                 src_ref=cbox.at[way, q], dst_ref=carry.at[p, chip],
-                send_sem=c_send.at[0], recv_sem=c_recv.at[p // ways],
+                send_sem=c_send.at[0], recv_sem=c_recv.at[min(p, parts - ways)],
                 device_id=place(q), device_id_type=MESH,
             ).start()
         carry[p, chip] = cbox[way, r]
@@ -447,26 +447,31 @@
 
     early = parts - ways
 
-    def wait_carry(side):
+    def wait_carry(first, count):
+        some_parts = pl.ds(first, count)
+
         @pl.when(core == owner)
         def _():
-            wait_all(carry.at[pl.ds(0, ways), pl.ds(0, span - 1)], c_recv.at[side])
+            wait_all(carry.at[some_parts, pl.ds(0, span - 1)], c_recv.at[first])
 
         @pl.when(core != owner)
         def _():
-            wait_all(carry.at[pl.ds(0, ways)], c_recv.at[side])
+            wait_all(carry.at[some_parts], c_recv.at[first])
 
     with jax.named_scope("wait_weight"):
         wait_all(weight_head.at[:, pl.ds(0, lead)], w_sem.at[0])
-    with jax.named_scope("wait_carry"):
-        for side in range(cores - 1):
-            wait_carry(side)
+    for p in range(early):
+        with jax.named_scope("wait_carry"):
+            wait_carry(p, 1)
+        if p < early - 1:
+            with jax.named_scope("finish"):
+                finish([p])
     with jax.named_scope("finish"):
-        finish(range(early))
+        finish([early - 1])
         for k in range(lead - 1):
             project(k, 0, cores - 1)
     with jax.named_scope("wait_carry"):
-        wait_carry(cores - 1)
+        wait_carry(early, ways)
     with jax.named_scope("project"):
         finish(range(early, parts), range(lead - 1, lead))
         for k in range(lead):
@@ -562,7 +567,7 @@
             dma((cores + 3,)), dma((2,)), dma((2,)), dma((2,)),
             dma((3,)), dma((1,)),
             dma((1,)), dma((parts,)), dma((1,)), dma((parts, groups)),
-            dma((1,)), dma((cores,)), pltpu.SemaphoreType.REGULAR,
+            dma((1,)), dma((parts - ways + 1,)), pltpu.SemaphoreType.REGULAR,
         ],
         compiler_params=pltpu.CompilerParams(
             collective_id=0, has_side_effects=True, vmem_limit_bytes=55 * 2**20

time: 19.9 us -> 19.9 us (level)
  no operation moved by 1% of the time
where the time goes in v11:
time: 19.9 us; the launch traced here: 19.7 us
  Pallas kernels  19.7 us (99%)
    pallas_call x1, Pallas kernels, shards(): pl.pallas_call(functools.partial(kernel, n, cores, breadth), out_shape=(p...  18.3 us
    pallas_call x1, Pallas kernels, shards(): pl.pallas_call(tail_kernel, out_shape=jax.ShapeDtypeStruct((tokens, depth...  1.43 us

profile of v11, /device:TPU:17, one launch (start us, length us, event | category | flops | bytes accessed | tf_op | source)
XLA Modules:
  0.0 19.7 jit_solution(2286510485564293510)
XLA Ops:
  0.0 18.3 %shard_map.82 = (bf16[256,3584]{1,0:T(8,128)(2,1)S(1)}, bf16[256,2048]{1,0:T(8,128)(2,1)S(1)}, bf16[2,1,1024,512]{3,2,1,0:T(8,128)(2,1)S(1)}) custom-call(bf16[256,2048]{1,0:T(8,128)(2,1)} %rec_hbm.1, bf16[256,2048]{1,0:T(8,128)(2,1)} %key_hbm.1, bf16[256,2048]{1,0:T(8,128)(2,1)} %val_hbm.1, bf16[256,2048]{1,0:T(8,128)(2,1)} %fade_hbm.1, ...), custom_call_target="tpu_custom_call" | custom-call | tf_op jit(solution)/shard_map/pallas_call | solution.py:539
  18.3 1.4 %shard_map.83 = bf16[256,4096]{1,0:T(8,128)(2,1)} custom-call(bf16[256,3584]{1,0:T(8,128)(2,1)S(1)} %get-tuple-element.8.done_ref, bf16[256,2048]{1,0:T(8,128)(2,1)S(1)} %get-tuple-element.9.gated_ref, bf16[2,1,1024,512]{3,2,1,0:T(8,128)(2,1)S(1)} %get-tuple-element.10.weight_ref), custom_call_target="tpu_custom_call" | custom-call | tf_op jit(solution)/shard_map/pallas_call | solution.py:576
